TPU v7x, 32 devices: a whole 2x2x4 slice. The times are simulated.
32 devices in a mesh: rel: 4 (over y, x), tgt: 8 (over z, core).
Axes of the slice: x: 2, y: 2, z: 4, core: 2. Of those that a mesh axis runs over, the one named last changes fastest.
Arguments:
- features: bfloat16 [2048, 768], P('tgt'), may hold values from -6 to 6
- weights: bfloat16 [8, 768, 768], P('rel'), may hold values from -0.109375 to 0.109375
- bias: float32 [768], replicated, may hold values from -3 to 3
- cotangent: bfloat16 [2048, 768], P('tgt'), may hold values from -1.0546875 to 1.0546875
- tile_values: int32 [8, 2048, 8, 128], P('rel', 'tgt'), may hold values from 0 to 3, as said below
- tile_count: int32 [8, 16], P('rel', 'tgt'), may hold values from 1 to 8, as said below
- tile_slot: int32 [8, 16, 8], P('rel', 'tgt'), may hold values from 0 to 7, as said below
- source_blocks: int32 [8, 8], replicated, may hold values from -1 to 1, as said below
Outputs:
- output: bfloat16 [2048, 768], P('tgt', 'rel')
- grad_weights: float32 [8, 768, 768], P('rel', 'tgt')
- grad_features: float32 [16, 128, 768], P('tgt', 'rel')
Inputs may be any that keep to these rules, and one draw needn't show every extreme that they name: `tile_values`: entries in tile slots at or beyond the live count are arbitrary and take no part. `tile_count`: every relation has some tile row of targets with all 8 slots live. `tile_slot`: every tile slot, live or not, names an owner for which the target block's entry of source_blocks is not -1. `source_blocks`: entry [t, o] is a block index within owner o's 2 blocks, or -1 where target block t reads nothing from o; entry [t, t] is never -1.
All inputs are finite; a program needn't handle non-finite values.
Results may differ from a plain program's by a relative error of at most 0.01.
Values may be sent and summed in bfloat16 or wider, within the bound.
A program may use at most 64 MiB of HBM per device.

v0:
```python
import functools

import jax
import jax.numpy as jnp
from jax import lax
from jax.experimental import pallas as pl
from jax.experimental.pallas import tpu as pltpu
from jax.sharding import PartitionSpec as P

MESH = pl.DeviceIdType.MESH
F32 = jnp.float32
BF16 = jnp.bfloat16


def aligned(start, size, multiple):
    return pl.ds(pl.multiple_of(start, multiple), size)


def is_one(condition):
    return condition.astype(jnp.int32).astype(F32)


def pack(value, first, width):
    half = value.shape[0] // 2
    return jnp.concatenate(
        [value[:half, first : first + width], value[half:, first : first + width]], axis=1
    )


def kernel(
    n, groups,
    table, counts, slots,
    feat, cot, bias, values_hbm, weights_hbm,
    out, grad_w, grad_f,
    weights, values, staged, partner_staged, masked, fetched, adj, scale, msg, msg_t, wg_own, adj_t, pre,
    pre_send, pre_recv, cot_own, active, bias_own, gp_all, gp, gm,
    part, part_recv, part_sum, part_back,
    wg_pair, wg_pair_recv, up_send, up_recv, down_send, down_recv,
    load_sem, a_send, a_recv, b_send, b_recv, p_send, p_recv, g_send, g_recv,
    d_send, d_recv, e_send, e_recv, w_send, w_recv, u_send, u_recv, v_send, v_recv,
):
    me = lax.axis_index("tgt")
    grp = lax.axis_index("rel")
    rows, width = feat.shape
    relations = weights.shape[0]
    slot_total = slots.shape[2]
    blk = values.shape[1] // (rows * slot_total) * values.shape[2]
    sections = rows // blk
    quarter = blk // groups
    share = width // groups
    chips = n // 2
    chip, core = me // 2, lax.rem(me, 2)

    def tgt(j):
        return lax.rem(chip + j // 2, chips) * 2 + lax.rem(core + lax.rem(j, 2), 2)

    def tgt_back(j):
        return lax.rem(chip + chips - j // 2, chips) * 2 + lax.rem(core + lax.rem(j, 2), 2)

    partner = chip * 2 + 1 - core
    row, column = grp // 2, lax.rem(grp, 2)
    beside = row * 2 + 1 - column
    above = (1 - row) * 2 + column

    def rel(i):
        return lax.rem(grp + i, groups)

    load_w = pltpu.make_async_copy(weights_hbm, weights, load_sem.at[0])
    load_v = pltpu.make_async_copy(values_hbm, values, load_sem.at[1])
    load_v.start()
    load_w.start()

    barrier = pltpu.get_barrier_semaphore()

    @pl.loop(1, n)
    def _(j):
        pl.semaphore_signal(barrier, inc=1, device_id=(grp, tgt(j)), device_id_type=MESH)

    for i in range(1, groups):
        pl.semaphore_signal(barrier, inc=1, device_id=(rel(i), me), device_id_type=MESH)

    @pl.loop(0, n)
    def _(t):
        total = jnp.zeros((quarter, width), F32)
        for k in range(sections):
            block = feat[aligned(k * blk + grp * quarter, quarter, quarter), :].astype(F32)
            total = total + block * is_one(table[t, me] == k)
        staged[t] = total.astype(BF16)

    def whole_block(t):
        total = jnp.zeros((blk, width), F32)
        for k in range(sections):
            total = total + feat[k * blk : (k + 1) * blk, :].astype(F32) * is_one(table[t, me] == k)
        return total.astype(BF16)

    fetched[aligned(me * blk, blk, blk), :] = whole_block(me)
    partner_staged[...] = whole_block(partner)
    pl.semaphore_wait(barrier, n - 1 + groups - 1)

    def fetch(j):
        return pltpu.make_async_remote_copy(
            src_ref=staged.at[tgt(j)],
            dst_ref=fetched.at[aligned(me * blk + grp * quarter, quarter, quarter), :],
            send_sem=a_send.at[j], recv_sem=a_recv.at[j],
            device_id=(grp, tgt(j)), device_id_type=MESH,
        )

    fetch_pair = pltpu.make_async_remote_copy(
        src_ref=partner_staged, dst_ref=fetched.at[aligned(me * blk, blk, blk), :],
        send_sem=a_send.at[1], recv_sem=a_recv.at[1],
        device_id=(grp, partner), device_id_type=MESH,
    )

    @pl.loop(2, n)
    def _(j):
        fetch(j).start()

    fetch_pair.start()

    def spread(j, way):
        size = quarter if way < 2 else quarter // 2
        source = (grp, grp, beside, above)[way]
        extra = quarter // 2 if way == 3 else 0
        peer = (beside, above, above, beside)[way]
        rows_at = aligned(tgt_back(j) * blk + source * quarter + extra, size, size)
        return pltpu.make_async_remote_copy(
            src_ref=fetched.at[rows_at, :], dst_ref=fetched.at[rows_at, :],
            send_sem=b_send.at[j, way], recv_sem=b_recv.at[j, way],
            device_id=(peer, me), device_id_type=MESH,
        )

    def pass_on(j):
        spread(j, 0).wait_recv()
        spread(j, 2).start()
        spread(j, 1).wait_recv()
        spread(j, 3).start()

    def arrive(j):
        fetch(j).wait_recv()
        spread(j, 0).start()
        spread(j, 1).start()

    load_v.wait()

    @pl.loop(0, relations * sections)
    def _(b):
        r, q = b // sections, lax.rem(b, sections)
        count = counts[r, q]

        def tile(s):
            start = (q * blk * slot_total) + s
            live = (s < count).astype(jnp.int32)
            return values[r, pl.ds(start, blk, stride=slot_total), :] * live

        total = jnp.zeros((blk, blk), jnp.int32)
        for s in range(slot_total):
            live_tile = tile(s)
            masked[s] = live_tile
            total = total + live_tile
        degree = jnp.sum(total.astype(F32), axis=1, keepdims=True)
        root = 1.0 / jnp.sqrt(jnp.maximum(degree, 1.0))
        scale[aligned(b * blk, blk, blk), :] = jnp.broadcast_to(root, (blk, 128))

        @pl.loop(0, n)
        def _(o):
            entry = jnp.zeros((blk, blk), jnp.int32)
            for s in range(slot_total):
                entry = entry + masked[s] * (slots[r, q, s] == o).astype(jnp.int32)
            wide = entry.astype(F32)
            adj[aligned(b * blk, blk, blk), aligned(o * blk, blk, blk)] = wide.astype(BF16)
            adj_t[aligned(o * blk, blk, blk), aligned(b * blk, blk, blk)] = wide.T.astype(BF16)

        arrive(b + 2)

    @pl.loop(relations * sections + 2, n)
    def _(j):
        arrive(j)
        pass_on(j - relations * sections)

    @pl.loop(n - relations * sections, n)
    def _(j):
        pass_on(j)

    load_w.wait()
    fetch_pair.wait_recv()

    @pl.loop(2, n)
    def _(j):
        spread(j, 2).wait_recv()
        spread(j, 3).wait_recv()

    tile_width = 256

    @pl.loop(0, width // tile_width)
    def _(c):
        at = aligned(c * tile_width, tile_width, tile_width)
        acc = jnp.dot(adj[...], fetched[:, at], preferred_element_type=F32)
        msg[:, at] = (acc * scale[:, 0:1]).astype(BF16)

    @pl.loop(0, width // tile_width)
    def _(c):
        at = aligned(c * tile_width, tile_width, tile_width)
        total = None
        for r in range(relations):
            part_r = jnp.dot(
                msg[r * rows : (r + 1) * rows, :], weights[r, :, at], preferred_element_type=F32
            )
            total = part_r if total is None else total + part_r
        pre[:, at] = total

    whole = pre[...]
    for k in range(groups):
        pre_send[k] = pack(whole, k * share, share).astype(BF16)

    piece_rows = rows // 4

    def reduce_pre(i, p):
        at = slice(p * piece_rows, (p + 1) * piece_rows)
        return pltpu.make_async_remote_copy(
            src_ref=pre_send.at[rel(i), at, :], dst_ref=pre_recv.at[i, at, :],
            send_sem=p_send.at[i, p], recv_sem=p_recv.at[i, p],
            device_id=(rel(i), me), device_id_type=MESH,
        )

    for p in range(2):
        for i in range(1, groups):
            reduce_pre(i, p).start()

    for r in range(relations):
        turned = msg[r * rows : (r + 1) * rows, :].astype(F32).T
        cut = turned.reshape(n, width // n, rows)
        for c in range(2):
            msg_t[r, c] = jnp.concatenate([cut[z * 2 + c] for z in range(chips)], axis=0).astype(BF16)

    for k in range(groups):
        @pl.when(grp == k)
        def _():
            cot_own[...] = pack(cot[...].astype(F32), k * share, share)
            piece = bias[...].reshape(1, width)[:, k * share : (k + 1) * share]
            bias_own[...] = jnp.concatenate([piece, piece], axis=1)

    def gather_gp(i, p):
        at = slice(p * piece_rows, (p + 1) * piece_rows)
        return pltpu.make_async_remote_copy(
            src_ref=gp_all.at[grp, at, :], dst_ref=gp_all.at[grp, at, :],
            send_sem=g_send.at[i, p], recv_sem=g_recv.at[i, p],
            device_id=(rel(i), me), device_id_type=MESH,
        )

    for p in range(2):
        at = slice(p * piece_rows, (p + 1) * piece_rows)
        total = pre_send[grp, at, :].astype(F32)
        for i in range(1, groups):
            reduce_pre(i, p).wait_recv()
            total = total + pre_recv[i, at, :].astype(F32)
        pre_act = total + bias_own[...]
        sigmoid = jax.nn.sigmoid(pre_act)
        derivative = sigmoid * (1.0 + pre_act * (1.0 - sigmoid))
        gp_all[grp, at, :] = (cot_own[at, :] * derivative).astype(BF16)
        for i in range(1, groups):
            gather_gp(i, p).start()
        active[at, :] = pre_act * sigmoid

    upright = active[...].T
    for h in range(2):
        out[:, h * (rows // 2) : (h + 1) * (rows // 2)] = upright[h * share : (h + 1) * share].astype(BF16)

    for p in range(2):
        for i in range(1, groups):
            gather_gp(i, p).wait_recv()
    half = rows // 2
    for h in range(2):
        gp[h * half : (h + 1) * half, :] = jnp.concatenate(
            [gp_all[k][:, h * share : (h + 1) * share].astype(F32) for k in range(groups)], axis=1
        ).astype(BF16)

    def weight_chunks(r, c):
        product = jnp.dot(msg_t[r, c], gp[...], preferred_element_type=F32)
        return product.reshape(chips, width // n, width)

    def pair(z):
        return pltpu.make_async_remote_copy(
            src_ref=wg_pair.at[z], dst_ref=wg_pair_recv.at[z],
            send_sem=w_send.at[z], recv_sem=w_recv.at[z],
            device_id=(grp, partner), device_id_type=MESH,
        )

    for r in range(relations):
        wg_pair[:, r] = weight_chunks(r, 1 - core).astype(BF16)

    @pl.loop(0, chips)
    def _(z):
        pair(z).start()

    for r in range(relations):
        wg_own[:, r] = weight_chunks(r, core)

    def climb(d):
        return pltpu.make_async_remote_copy(
            src_ref=up_send.at[d], dst_ref=up_recv.at[d],
            send_sem=u_send.at[d], recv_sem=u_recv.at[d],
            device_id=(grp, jnp.minimum(chip + 1, chips - 1) * 2 + core), device_id_type=MESH,
        )

    def descend(d):
        return pltpu.make_async_remote_copy(
            src_ref=down_send.at[d], dst_ref=down_recv.at[d],
            send_sem=v_send.at[d], recv_sem=v_recv.at[d],
            device_id=(grp, jnp.maximum(chip - 1, 0) * 2 + core), device_id_type=MESH,
        )

    def chip_sum(r, z):
        return wg_own[z, r] + wg_pair_recv[z, r].astype(F32)

    def line_step(step):
        @pl.when(step >= chip)
        def _():
            d = chips - 1 - step + chip

            @pl.when(chip > 0)
            def _():
                climb(d).wait_recv()
                for r in range(relations):
                    up_send[d, r] = (chip_sum(r, d) + up_recv[d, r].astype(F32)).astype(BF16)

            @pl.when(chip == 0)
            def _():
                for r in range(relations):
                    up_send[d, r] = chip_sum(r, d).astype(BF16)

            climb(d).start()

        @pl.when(step >= chips - 1 - chip)
        def _():
            d = step - chips + 1 + chip

            @pl.when(chip < chips - 1)
            def _():
                descend(d).wait_recv()
                for r in range(relations):
                    down_send[d, r] = (chip_sum(r, d) + down_recv[d, r].astype(F32)).astype(BF16)

            @pl.when(chip == chips - 1)
            def _():
                for r in range(relations):
                    down_send[d, r] = chip_sum(r, d).astype(BF16)

            descend(d).start()

    @pl.loop(0, chips)
    def _(z):
        pair(z).wait_recv()

    line_step(0)

    @pl.loop(0, width // tile_width)
    def _(c):
        at = aligned(c * tile_width, tile_width, tile_width)
        for r in range(relations):
            rows_r = slice(r * rows, (r + 1) * rows)
            grads = lax.dot_general(
                gp[...], weights[r, at, :],
                (((1,), (1,)), ((), ())), preferred_element_type=F32,
            )
            gm[rows_r, at] = (grads * scale[rows_r, 0:1]).astype(BF16)

    def reduce_part(o, i):
        return pltpu.make_async_remote_copy(
            src_ref=part.at[o, aligned(rel(i) * quarter, quarter, quarter), :],
            dst_ref=part_recv.at[i, o],
            send_sem=d_send.at[o, i], recv_sem=d_recv.at[o, i],
            device_id=(rel(i), me), device_id_type=MESH,
        )

    @pl.loop(1, chips + 1)
    def _(e):
        z = lax.rem(chip + e, chips)
        product = jnp.dot(
            adj_t[aligned(z * 2 * blk, 2 * blk, blk), :], gm[...], preferred_element_type=F32
        )
        for v in range(2):
            o = z * 2 + v
            part[o] = product[v * blk : (v + 1) * blk].astype(BF16)
            for i in range(1, groups):
                reduce_part(o, i).start()

    def give_back(j):
        return pltpu.make_async_remote_copy(
            src_ref=part_sum.at[tgt(j)], dst_ref=part_back.at[me],
            send_sem=e_send.at[j], recv_sem=e_recv.at[j],
            device_id=(grp, tgt(j)), device_id_type=MESH,
        )

    def reduced(o):
        total = part[o, aligned(grp * quarter, quarter, quarter), :].astype(F32)
        for i in range(1, groups):
            reduce_part(o, i).wait_recv()
            total = total + part_recv[i, o].astype(F32)
        return total.astype(BF16)

    def send_reduced(j):
        part_sum[tgt(j)] = reduced(tgt(j))
        give_back(j).start()

    @pl.loop(1, chips - 1)
    def _(step):
        line_step(step)
        send_reduced(2 * step)
        send_reduced(2 * step + 1)

    for r in range(relations):
        grad_w[r] = chip_sum(r, chip)

    send_reduced(n - 2)
    send_reduced(n - 1)
    send_reduced(1)
    part_back[me] = reduced(me)

    @pl.when(chip > 0)
    def _():
        climb(chip).wait_recv()
        for r in range(relations):
            grad_w[r] = grad_w[r] + up_recv[chip, r].astype(F32)

    @pl.when(chip < chips - 1)
    def _():
        descend(chip).wait_recv()
        for r in range(relations):
            grad_w[r] = grad_w[r] + down_recv[chip, r].astype(F32)

    @pl.loop(1, n)
    def _(j):
        give_back(j).wait_recv()

    for k in range(sections):
        grad_f[k] = jnp.zeros((quarter, width), F32)

    @pl.loop(0, n)
    def _(t):
        wanted = table[t, me]
        addend = part_back[t].astype(F32)
        for k in range(sections):
            grad_f[k] = grad_f[k] + addend * is_one(wanted == k)

    fetch_pair.wait_send()

    @pl.loop(2, n)
    def _(j):
        fetch(j).wait_send()
        for way in range(4):
            spread(j, way).wait_send()

    @pl.loop(1, n)
    def _(j):
        give_back(j).wait_send()

    for i in range(1, groups):
        for p in range(2):
            reduce_pre(i, p).wait_send()
            gather_gp(i, p).wait_send()

    @pl.loop(0, n)
    def _(o):
        for i in range(1, groups):
            reduce_part(o, i).wait_send()

    @pl.loop(0, chips)
    def _(z):
        pair(z).wait_send()

        @pl.when(z > chip)
        def _():
            climb(z).wait_send()

        @pl.when(z < chip)
        def _():
            descend(z).wait_send()


def hand_over(out_in, grad_w_in, grad_f_in, out, grad_w, grad_f):
    out[...] = out_in[...]
    grad_w[...] = grad_w_in[...]
    grad_f[...] = grad_f_in[...]


def per_device(
    n, groups,
    features, weights, bias, cotangent, tile_values, tile_count, tile_slot, source_blocks,
):
    rows, width = features.shape
    relations, _, slot_total, blk = tile_values.shape
    sections = rows // blk
    quarter, share, chunk, chips = blk // groups, width // groups, width // n, n // 2
    half = rows // 2
    vmem = pl.BlockSpec(memory_space=pltpu.VMEM)
    smem = pl.BlockSpec(memory_space=pltpu.SMEM)
    anywhere = pl.BlockSpec(memory_space=pl.ANY)
    dma = pltpu.SemaphoreType.DMA
    out, grad_w, grad_f = pl.pallas_call(
        functools.partial(kernel, n, groups),
        out_shape=(
            jax.ShapeDtypeStruct((share, rows), BF16),
            jax.ShapeDtypeStruct((relations, chunk, width), F32),
            jax.ShapeDtypeStruct((sections, quarter, width), F32),
        ),
        in_specs=[smem, smem, smem, vmem, vmem, vmem, anywhere, anywhere],
        out_specs=(vmem, vmem, vmem),
        scratch_shapes=[
            pltpu.VMEM((relations, width, width), BF16),
            pltpu.VMEM((relations, rows * slot_total, blk), jnp.int32),
            pltpu.VMEM((n, quarter, width), BF16),
            pltpu.VMEM((blk, width), BF16),
            pltpu.VMEM((slot_total, blk, blk), jnp.int32),
            pltpu.VMEM((n * blk, width), BF16),
            pltpu.VMEM((relations * rows, n * blk), BF16),
            pltpu.VMEM((relations * rows, 128), F32),
            pltpu.VMEM((relations * rows, width), BF16),
            pltpu.VMEM((relations, 2, chips * chunk, rows), BF16),
            pltpu.VMEM((chips, relations, chunk, width), F32),
            pltpu.VMEM((n * blk, relations * rows), BF16),
            pltpu.VMEM((rows, width), F32),
            pltpu.VMEM((groups, half, 2 * share), BF16),
            pltpu.VMEM((groups, half, 2 * share), BF16),
            pltpu.VMEM((half, 2 * share), F32),
            pltpu.VMEM((half, 2 * share), F32),
            pltpu.VMEM((1, 2 * share), F32),
            pltpu.VMEM((groups, half, 2 * share), BF16),
            pltpu.VMEM((rows, width), BF16),
            pltpu.VMEM((relations * rows, width), BF16),
            pltpu.VMEM((n, blk, width), BF16),
            pltpu.VMEM((groups, n, quarter, width), BF16),
            pltpu.VMEM((n, quarter, width), BF16),
            pltpu.VMEM((n, quarter, width), BF16),
            pltpu.VMEM((chips, relations, chunk, width), BF16),
            pltpu.VMEM((chips, relations, chunk, width), BF16),
            pltpu.VMEM((chips, relations, chunk, width), BF16),
            pltpu.VMEM((chips, relations, chunk, width), BF16),
            pltpu.VMEM((chips, relations, chunk, width), BF16),
            pltpu.VMEM((chips, relations, chunk, width), BF16),
            dma((2,)),
            dma((n,)), dma((n,)),
            dma((n, 4)), dma((n, 4)),
            dma((groups, 2)), dma((groups, 2)),
            dma((groups, 2)), dma((groups, 2)),
            dma((n, groups)), dma((n, groups)),
            dma((n,)), dma((n,)),
            dma((chips,)), dma((chips,)),
            dma((chips,)), dma((chips,)),
            dma((chips,)), dma((chips,)),
        ],
        compiler_params=pltpu.CompilerParams(
            collective_id=0, has_side_effects=True, vmem_limit_bytes=60 << 20
        ),
        name="layer",
    )(
        source_blocks, tile_count, tile_slot,
        features, cotangent, bias,
        tile_values.reshape(relations, rows * slot_total, blk), weights,
    )
    results = (out, grad_w, grad_f)
    out, grad_w, grad_f = pl.pallas_call(
        hand_over,
        out_shape=tuple(jax.ShapeDtypeStruct(x.shape, x.dtype) for x in results),
        in_specs=[vmem] * 3,
        out_specs=(vmem,) * 3,
        name="hand_over",
    )(*results)
    return (out.T, grad_w, grad_f)


def solution(mesh):
    placed = (
        P("tgt", None),
        P("rel", None, None),
        P(),
        P("tgt", None),
        P("rel", "tgt", None, None),
        P("rel", "tgt"),
        P("rel", "tgt", None),
        P(),
    )
    return jax.shard_map(
        functools.partial(per_device, mesh.shape["tgt"], mesh.shape["rel"]),
        mesh=mesh,
        in_specs=placed,
        out_specs=(P("tgt", "rel"), P("rel", "tgt", None), P("tgt", "rel", None)),
        check_vma=False,
    )
```

profile of v0, /device:TPU:0, one launch (start us, length us, event | category | flops | bytes accessed | tf_op | source)
XLA Modules:
  0.0 78.5 jit_solution(8882856847197844765)
XLA Ops:
  0.6 75.8 %layer.1 = (bf16[192,256]{1,0:T(8,128)(2,1)}, f32[2,96,768]{2,1,0:T(8,128)}, f32[2,32,768]{2,1,0:T(8,128)}) custom-call(s32[8,8]{1,0:T(8,128)} %table.1, s32[2,2]{1,0:T(2,128)} %counts.1, s32[2,2,8]{2,1,0:T(2,128)} %slots.1, bf16[256,768]{1,0:T(8,128)(2,1)} %feat.1, bf16[256,768]{1,0:T(8,128)(2,1)} %cot.1, f32[768]{0:T(1024)} %bias.1, ...), custom_call_target="tpu_custom_call" | custom-call | tf_op jit(solution)/shard_map/layer/pallas_call | solution.py:499
  76.5 2.1 %hand_over.1 = (bf16[192,256]{1,0:T(8,128)(2,1)}, f32[2,96,768]{2,1,0:T(8,128)}, f32[2,32,768]{2,1,0:T(8,128)}) custom-call(bf16[192,256]{1,0:T(8,128)(2,1)} %get-tuple-element.9.out_in, f32[2,96,768]{2,1,0:T(8,128)} %get-tuple-element.10.grad_w_in, f32[2,32,768]{2,1,0:T(8,128)} %get-tuple-element.11.grad_f_in), custom_call_target="tpu_custom_call" | custom-call | tf_op jit(solution)/shard_map/hand_over/pallas_call | solution.py:561
where the time goes:
time: 78.7 us; the launch traced here: 78.5 us
  Pallas kernels  77.9 us (99%)
    pallas_call x1, Pallas kernels, per_device(): pl.pallas_call(functools.partial(kernel, n, groups), out_shape=(jax.Shape...  75.8 us
    pallas_call x1, Pallas kernels, per_device(): pl.pallas_call(hand_over, out_shape=tuple((jax.ShapeDtypeStruct(x.shape,...  2.08 us

commit v1 on v0

v1 whole, which is shorter than its diff:
```python
import functools

import jax
import jax.numpy as jnp
from jax import lax
from jax.experimental import pallas as pl
from jax.experimental.pallas import tpu as pltpu
from jax.sharding import PartitionSpec as P

MESH = pl.DeviceIdType.MESH
F32 = jnp.float32
BF16 = jnp.bfloat16


def aligned(start, size, multiple):
    return pl.ds(pl.multiple_of(start, multiple), size)


def is_one(condition):
    return condition.astype(jnp.int32).astype(F32)


def pack(value, first, width):
    half = value.shape[0] // 2
    return jnp.concatenate(
        [value[:half, first : first + width], value[half:, first : first + width]], axis=1
    )


def drain(view, semaphore):
    pltpu.make_async_copy(view, view, semaphore).wait()


def kernel(
    n, groups,
    table, counts, slots,
    feat, cot, bias, values_hbm, weights_hbm,
    out_hbm, grad_w_hbm, grad_f_hbm,
    out, grad_w, grad_f, out_sem,
    weights, values, gathered, partner_staged, masked, masked_t, fetched, adj, scale, msg, msg_t, wg_own, adj_t, pre,
    pre_send, pre_recv, cot_own, active, bias_own, gp_all, gp, gm,
    part, part_recv, part_sum, part_back,
    wg_pair, wg_pair_recv, up_send, up_recv, down_send, down_recv,
    load_sem, pair_sem, sent_sem, spread_sem, back_sem,
    a_recv, b_recv, p_recv, g_recv, d_recv, w_recv, u_recv, v_recv,
):
    me = lax.axis_index("tgt")
    grp = lax.axis_index("rel")
    sections, _, quarter, width = feat.shape
    blk = quarter * groups
    rows = sections * blk
    relations = weights.shape[0]
    slot_total = slots.shape[2]
    share = width // groups
    chips = n // 2
    chip, core = me // 2, lax.rem(me, 2)

    def tgt(j):
        return lax.rem(chip + j // 2, chips) * 2 + lax.rem(core + lax.rem(j, 2), 2)

    below, above_me = chip, chips - 1 - chip
    both = jnp.minimum(below, above_me)

    def near(j):
        k = j // 2 - 1
        two_sided = jnp.where(lax.rem(k, 2) == 0, chip + k // 2 + 1, chip - k // 2 - 1)
        distance = k - both + 1
        one_sided = jnp.where(above_me > below, chip + distance, chip - distance)
        return jnp.where(k < 2 * both, two_sided, one_sided) * 2 + lax.rem(core + lax.rem(j, 2), 2)

    partner = chip * 2 + 1 - core
    row, column = grp // 2, lax.rem(grp, 2)
    beside = row * 2 + 1 - column
    above = (1 - row) * 2 + column

    square = groups == 4

    def rel(i):
        if square:
            return (grp, beside, above, (1 - row) * 2 + 1 - column)[i]
        return lax.rem(grp + i, groups)

    load_w = pltpu.make_async_copy(weights_hbm, weights, load_sem.at[0])
    load_v = pltpu.make_async_copy(values_hbm, values, load_sem.at[1])
    load_v.start()
    load_w.start()

    barrier = pltpu.get_barrier_semaphore()

    @pl.loop(1, n)
    def _(j):
        pl.semaphore_signal(barrier, inc=1, device_id=(grp, tgt(j)), device_id_type=MESH)

    for i in range(1, groups):
        pl.semaphore_signal(barrier, inc=1, device_id=(rel(i), me), device_id_type=MESH)

    def whole_block(t):
        total = jnp.zeros((blk, width), F32)
        for k in range(sections):
            total = total + feat[k].reshape(blk, width).astype(F32) * is_one(table[t, me] == k)
        return total.astype(BF16)

    fetched[aligned(me * blk, blk, blk), :] = whole_block(me)
    partner_staged[...] = whole_block(partner)
    pl.semaphore_wait(barrier, n - 1 + groups - 1)

    cut = width // 2

    def columns(h):
        return aligned(h * cut, cut, 128)

    def climb_rows(o, h, source):
        return pltpu.make_async_remote_copy(
            src_ref=source, dst_ref=gathered.at[o, :, :, columns(h)],
            send_sem=sent_sem.at[0], recv_sem=a_recv.at[o, h],
            device_id=(grp, jnp.minimum(chip + 1, chips - 1) * 2 + core), device_id_type=MESH,
        )

    def descend_rows(o, h, source):
        return pltpu.make_async_remote_copy(
            src_ref=source, dst_ref=gathered.at[o, :, :, columns(h)],
            send_sem=sent_sem.at[0], recv_sem=a_recv.at[o, h],
            device_id=(grp, jnp.maximum(chip - 1, 0) * 2 + core), device_id_type=MESH,
        )

    def across_rows(o, h):
        return pltpu.make_async_remote_copy(
            src_ref=gathered.at[o, :, :, columns(h)], dst_ref=gathered.at[o, :, :, columns(h)],
            send_sem=sent_sem.at[0], recv_sem=a_recv.at[o, h],
            device_id=(grp, partner), device_id_type=MESH,
        )

    fetch_pair = pltpu.make_async_remote_copy(
        src_ref=partner_staged, dst_ref=fetched.at[aligned(me * blk, blk, blk), :],
        send_sem=pair_sem.at[0], recv_sem=pair_sem.at[1],
        device_id=(grp, partner), device_id_type=MESH,
    )

    for h in range(2):
        @pl.when(chip < chips - 1)
        def _():
            climb_rows(me, h, feat.at[:, grp, :, columns(h)]).start()

        @pl.when(chip > 0)
        def _():
            descend_rows(me, h, feat.at[:, grp, :, columns(h)]).start()

    fetch_pair.start()

    sent = range(4) if square else range(groups - 1)

    def spread(j, h, way):
        if square:
            size = quarter if way < 2 else quarter // 2
            source = (grp, grp, beside, above)[way]
            extra = quarter // 2 if way == 3 else 0
            peer = (beside, above, above, beside)[way]
        else:
            size, source, extra, peer = quarter, grp, 0, rel(way + 1)
        rows_at = aligned(near(j) * blk + source * quarter + extra, size, size)
        return pltpu.make_async_remote_copy(
            src_ref=fetched.at[rows_at, columns(h)], dst_ref=fetched.at[rows_at, columns(h)],
            send_sem=sent_sem.at[1],
            recv_sem=b_recv.at[j, h, way] if square and way < 2 else spread_sem,
            device_id=(peer, me), device_id_type=MESH,
        )

    first_hop = sent[:2] if square else sent

    def event(e):
        inner = lax.rem(e, 4)
        paired = e < 4 * both
        k = jnp.where(paired, e // 4 * 2 + 1 + lax.rem(inner, 2), e // 2 + 1)
        return k, jnp.where(paired, inner // 2, lax.rem(e, 2))

    def pass_on(e, side):
        k, h = event(e)
        j = 2 * k + side
        if not square:
            return
        spread(j, h, 0).wait_recv()
        spread(j, h, 2).start()
        spread(j, h, 1).wait_recv()
        spread(j, h, 3).start()

    def placed(j, h):
        o = near(j)
        total = jnp.zeros((quarter, cut), F32)
        for k in range(sections):
            total = total + gathered[o, k, :, columns(h)].astype(F32) * is_one(table[me, o] == k)
        fetched[aligned(o * blk + grp * quarter, quarter, quarter), columns(h)] = total.astype(BF16)
        for way in first_hop:
            spread(j, h, way).start()

    def arrive(e):
        k, h = event(e)
        o = near(2 * k)
        across_rows(o, h).wait_recv()

        @pl.when((o < me) & (chip < chips - 1))
        def _():
            climb_rows(o, h, gathered.at[o, :, :, columns(h)]).start()

        @pl.when((o > me) & (chip > 0))
        def _():
            descend_rows(o, h, gathered.at[o, :, :, columns(h)]).start()

        across_rows(o, h).start()
        placed(2 * k, h)

    def arrive_across(e):
        k, h = event(e)
        across_rows(near(2 * k + 1), h).wait_recv()
        placed(2 * k + 1, h)

    load_v.wait()

    def adjacency(b):
        r, q = b // sections, lax.rem(b, sections)
        count = counts[r, q]
        total = jnp.zeros((blk, blk), F32)
        for s in range(slot_total):
            start = (q * blk * slot_total) + s
            tile = values[r, pl.ds(start, blk, stride=slot_total), :].astype(F32) * is_one(s < count)
            masked[s] = tile.astype(BF16)
            masked_t[s] = tile.T.astype(BF16)
            total = total + tile
        degree = jnp.sum(total, axis=1, keepdims=True)
        root = 1.0 / jnp.sqrt(jnp.maximum(degree, 1.0))
        scale[aligned(b * blk, blk, blk), :] = jnp.broadcast_to(root, (blk, 128))

        @pl.loop(0, n)
        def _(o):
            entry = jnp.zeros((blk, blk), BF16)
            entry_t = jnp.zeros((blk, blk), BF16)
            for s in range(slot_total):
                here = jnp.full((blk, blk), is_one(slots[r, q, s] == o), F32).astype(BF16)
                entry = entry + masked[s] * here
                entry_t = entry_t + masked_t[s] * here
            adj[aligned(b * blk, blk, blk), aligned(o * blk, blk, blk)] = entry
            adj_t[aligned(o * blk, blk, blk), aligned(b * blk, blk, blk)] = entry_t

    blocks = relations * sections

    @pl.loop(0, blocks // 2)
    def _(b):
        adjacency(b)

    events = 2 * (chips - 1)
    arrive(0)
    arrive(1)

    @pl.loop(0, blocks // 2)
    def _(b):
        adjacency(blocks // 2 + b)
        arrive_across(b)
        arrive(2 + b)

    @pl.loop(blocks // 2 + 2, events)
    def _(e):
        arrive(e)
        arrive_across(e - 2)

    pass_on(0, 0)
    arrive_across(events - 2)
    pass_on(0, 1)
    arrive_across(events - 1)

    @pl.loop(1, events)
    def _(e):
        pass_on(e, 0)
        pass_on(e, 1)

    load_w.wait()
    fetch_pair.wait_recv()

    late = n - 2 if square else (n - 2) * (groups - 1)
    drain(fetched.at[: late * quarter, :], spread_sem)

    tile_width = 256

    @pl.loop(0, width // tile_width)
    def _(c):
        at = aligned(c * tile_width, tile_width, tile_width)
        acc = jnp.dot(adj[...], fetched[:, at], preferred_element_type=F32)
        msg[:, at] = (acc * scale[:, 0:1]).astype(BF16)

    @pl.loop(0, width // tile_width)
    def _(c):
        at = aligned(c * tile_width, tile_width, tile_width)
        total = None
        for r in range(relations):
            part_r = jnp.dot(
                msg[r * rows : (r + 1) * rows, :], weights[r, :, at], preferred_element_type=F32
            )
            total = part_r if total is None else total + part_r
        pre[:, at] = total

    whole = pre[...]
    for k in range(groups):
        pre_send[k] = pack(whole, k * share, share).astype(BF16)

    piece_rows = rows // 4

    def reduce_pre(i, p):
        at = slice(p * piece_rows, (p + 1) * piece_rows)
        return pltpu.make_async_remote_copy(
            src_ref=pre_send.at[rel(i), at, :], dst_ref=pre_recv.at[i, at, :],
            send_sem=sent_sem.at[2], recv_sem=p_recv.at[p],
            device_id=(rel(i), me), device_id_type=MESH,
        )

    for p in range(2):
        for i in range(1, groups):
            reduce_pre(i, p).start()

    for r in range(relations):
        turned = msg[r * rows : (r + 1) * rows, :].astype(F32).T
        sliced = turned.reshape(n, width // n, rows)
        for c in range(2):
            msg_t[r, c] = jnp.concatenate([sliced[z * 2 + c] for z in range(chips)], axis=0).astype(BF16)

    for k in range(groups):
        @pl.when(grp == k)
        def _():
            cot_own[...] = pack(cot[...].astype(F32), k * share, share)
            piece = bias[...].reshape(1, width)[:, k * share : (k + 1) * share]
            bias_own[...] = jnp.concatenate([piece, piece], axis=1)

    def gather_gp(i, p):
        at = slice(p * piece_rows, (p + 1) * piece_rows)
        return pltpu.make_async_remote_copy(
            src_ref=gp_all.at[grp, at, :], dst_ref=gp_all.at[grp, at, :],
            send_sem=sent_sem.at[3], recv_sem=g_recv.at[p],
            device_id=(rel(i), me), device_id_type=MESH,
        )

    for p in range(2):
        at = slice(p * piece_rows, (p + 1) * piece_rows)
        total = pre_send[grp, at, :].astype(F32)
        drain(pre_recv.at[1:groups, at, :], p_recv.at[p])
        for i in range(1, groups):
            total = total + pre_recv[i, at, :].astype(F32)
        pre_act = total + bias_own[...]
        sigmoid = jax.nn.sigmoid(pre_act)
        derivative = sigmoid * (1.0 + pre_act * (1.0 - sigmoid))
        gp_all[grp, at, :] = (cot_own[at, :] * derivative).astype(BF16)
        for i in range(1, groups):
            gather_gp(i, p).start()
        active[at, :] = pre_act * sigmoid

    upright = active[...].T
    for h in range(2):
        out[:, h * (rows // 2) : (h + 1) * (rows // 2)] = upright[h * share : (h + 1) * share].astype(BF16)

    save_out = pltpu.make_async_copy(out, out_hbm, out_sem.at[0])
    save_w = pltpu.make_async_copy(grad_w, grad_w_hbm, out_sem.at[1])
    save_f = pltpu.make_async_copy(grad_f, grad_f_hbm, out_sem.at[2])
    save_out.start()

    for p in range(2):
        drain(pre_recv.at[1:groups, p * piece_rows : (p + 1) * piece_rows, :], g_recv.at[p])
    half = rows // 2
    for h in range(2):
        gp[h * half : (h + 1) * half, :] = jnp.concatenate(
            [gp_all[k][:, h * share : (h + 1) * share].astype(F32) for k in range(groups)], axis=1
        ).astype(BF16)

    def weight_chunks(r, c):
        product = jnp.dot(msg_t[r, c], gp[...], preferred_element_type=F32)
        return product.reshape(chips, width // n, width)

    def pair(z):
        return pltpu.make_async_remote_copy(
            src_ref=wg_pair.at[z], dst_ref=wg_pair_recv.at[z],
            send_sem=sent_sem.at[4], recv_sem=w_recv.at[z],
            device_id=(grp, partner), device_id_type=MESH,
        )

    for r in range(relations):
        wg_pair[:, r] = weight_chunks(r, 1 - core).astype(BF16)

    upper = chip >= chips // 2

    def order(i):
        return jnp.where(upper, i, chips - 1 - i)

    @pl.loop(0, chips)
    def _(i):
        pair(order(i)).start()

    for r in range(relations):
        wg_own[:, r] = weight_chunks(r, core)

    @pl.loop(0, width // tile_width)
    def _(c):
        at = aligned(c * tile_width, tile_width, tile_width)
        for r in range(relations):
            rows_r = slice(r * rows, (r + 1) * rows)
            grads = lax.dot_general(
                gp[...], weights[r, at, :],
                (((1,), (1,)), ((), ())), preferred_element_type=F32,
            )
            gm[rows_r, at] = (grads * scale[rows_r, 0:1]).astype(BF16)

    def climb(d, r):
        return pltpu.make_async_remote_copy(
            src_ref=up_send.at[d, r], dst_ref=up_recv.at[d, r],
            send_sem=sent_sem.at[5], recv_sem=u_recv.at[d, r],
            device_id=(grp, jnp.minimum(chip + 1, chips - 1) * 2 + core), device_id_type=MESH,
        )

    def descend(d, r):
        return pltpu.make_async_remote_copy(
            src_ref=down_send.at[d, r], dst_ref=down_recv.at[d, r],
            send_sem=sent_sem.at[5], recv_sem=v_recv.at[d, r],
            device_id=(grp, jnp.maximum(chip - 1, 0) * 2 + core), device_id_type=MESH,
        )

    def chip_sum(r, z):
        return wg_own[z, r] + wg_pair_recv[z, r].astype(F32)

    @pl.loop(0, chips)
    def _(i):
        z = order(i)
        pair(z).wait_recv()

        @pl.when((chip == 0) & (z > 0))
        def _():
            for r in range(relations):
                up_send[z, r] = chip_sum(r, z).astype(BF16)
                climb(z, r).start()

        @pl.when((chip == chips - 1) & (z < chips - 1))
        def _():
            for r in range(relations):
                down_send[z, r] = chip_sum(r, z).astype(BF16)
                descend(z, r).start()

    pieces = (chips - 1) * relations

    def line_piece(step):
        up = step - (chip - 1)
        d = chips - 1 - up // relations
        r = lax.rem(up, relations)

        @pl.when((chip > 0) & (up >= 0) & (up < pieces) & (d > chip))
        def _():
            climb(d, r).wait_recv()
            up_send[d, r] = (chip_sum(r, d) + up_recv[d, r].astype(F32)).astype(BF16)
            climb(d, r).start()

        down = step - (chips - 2 - chip)
        f = down // relations
        g = lax.rem(down, relations)

        @pl.when((chip < chips - 1) & (down >= 0) & (down < pieces) & (f < chip))
        def _():
            descend(f, g).wait_recv()
            down_send[f, g] = (chip_sum(g, f) + down_recv[f, g].astype(F32)).astype(BF16)
            descend(f, g).start()

    def reduce_part(o, i):
        return pltpu.make_async_remote_copy(
            src_ref=part.at[o, aligned(rel(i) * quarter, quarter, quarter), :],
            dst_ref=part_recv.at[i, o],
            send_sem=sent_sem.at[6], recv_sem=d_recv.at[o],
            device_id=(rel(i), me), device_id_type=MESH,
        )

    @pl.loop(1, chips + 1)
    def _(e):
        z = lax.rem(chip + e, chips)
        product = jnp.dot(
            adj_t[aligned(z * 2 * blk, 2 * blk, blk), :], gm[...], preferred_element_type=F32
        )
        for v in range(2):
            o = z * 2 + v
            part[o] = product[v * blk : (v + 1) * blk].astype(BF16)
            for i in range(1, groups):
                reduce_part(o, i).start()

    def give_back(j):
        return pltpu.make_async_remote_copy(
            src_ref=part_sum.at[tgt(j)], dst_ref=part_back.at[me],
            send_sem=sent_sem.at[7], recv_sem=back_sem,
            device_id=(grp, tgt(j)), device_id_type=MESH,
        )

    def reduced(o):
        total = part[o, aligned(grp * quarter, quarter, quarter), :].astype(F32)
        drain(part_recv.at[1:groups, o], d_recv.at[o])
        for i in range(1, groups):
            total = total + part_recv[i, o].astype(F32)
        return total.astype(BF16)

    def send_reduced(j):
        part_sum[tgt(j)] = reduced(tgt(j))
        give_back(j).start()

    @pl.loop(0, pieces + chips - 2)
    def _(step):
        line_piece(step)

        @pl.when(step + 2 < n)
        def _():
            send_reduced(step + 2)

    send_reduced(1)
    part_back[me] = reduced(me)

    for r in range(relations):
        grad_w[r] = chip_sum(r, chip)

    @pl.when(chip > 0)
    def _():
        for r in range(relations):
            climb(chip, r).wait_recv()
            grad_w[r] = grad_w[r] + up_recv[chip, r].astype(F32)

    @pl.when(chip < chips - 1)
    def _():
        for r in range(relations):
            descend(chip, r).wait_recv()
            grad_w[r] = grad_w[r] + down_recv[chip, r].astype(F32)

    save_w.start()

    drain(part_sum.at[: n - 1], back_sem)

    for k in range(sections):
        grad_f[k] = jnp.zeros((quarter, width), F32)

    @pl.loop(0, n)
    def _(t):
        wanted = table[t, me]
        addend = part_back[t].astype(F32)
        for k in range(sections):
            grad_f[k] = grad_f[k] + addend * is_one(wanted == k)

    save_f.start()

    fetch_pair.wait_send()
    at_end = (chip == 0) | (chip == chips - 1)

    @pl.when(at_end)
    def _():
        drain(gathered.at[:chips], sent_sem.at[0])

    @pl.when(jnp.logical_not(at_end))
    def _():
        drain(gathered, sent_sem.at[0])

    drain(fetched.at[: (n - 2) * (groups - 1) * quarter, :], sent_sem.at[1])
    drain(pre_recv.at[1:groups], sent_sem.at[2])
    drain(pre_recv.at[1:groups], sent_sem.at[3])
    drain(wg_pair, sent_sem.at[4])
    drain(up_send.at[: chips - 1], sent_sem.at[5])
    drain(part_recv.at[1:groups], sent_sem.at[6])
    drain(part_sum.at[: n - 1], sent_sem.at[7])
    save_out.wait()
    save_w.wait()
    save_f.wait()


def hand_over(out_in, grad_w_in, grad_f_in, out, grad_w, grad_f):
    out[...] = out_in[...]
    grad_w[...] = grad_w_in[...]
    grad_f[...] = grad_f_in[...]


def per_device(
    n, groups,
    features, weights, bias, cotangent, tile_values, tile_count, tile_slot, source_blocks,
):
    rows, width = features.shape
    relations, _, slot_total, blk = tile_values.shape
    sections = rows // blk
    quarter, share, chunk, chips = blk // groups, width // groups, width // n, n // 2
    half = rows // 2
    vmem = pl.BlockSpec(memory_space=pltpu.VMEM)
    smem = pl.BlockSpec(memory_space=pltpu.SMEM)
    anywhere = pl.BlockSpec(memory_space=pl.ANY)
    dma = pltpu.SemaphoreType.DMA
    out, grad_w, grad_f = pl.pallas_call(
        functools.partial(kernel, n, groups),
        out_shape=(
            jax.ShapeDtypeStruct((share, rows), BF16),
            jax.ShapeDtypeStruct((relations, chunk, width), F32),
            jax.ShapeDtypeStruct((sections, quarter, width), F32),
        ),
        in_specs=[smem, smem, smem, vmem, vmem, vmem, anywhere, anywhere],
        out_specs=(anywhere, anywhere, anywhere),
        scratch_shapes=[
            pltpu.VMEM((share, rows), BF16),
            pltpu.VMEM((relations, chunk, width), F32),
            pltpu.VMEM((sections, quarter, width), F32),
            dma((3,)),
            pltpu.VMEM((relations, width, width), BF16),
            pltpu.VMEM((relations, rows * slot_total, blk), jnp.int32),
            pltpu.VMEM((n, sections, quarter, width), BF16),
            pltpu.VMEM((blk, width), BF16),
            pltpu.VMEM((slot_total, blk, blk), BF16),
            pltpu.VMEM((slot_total, blk, blk), BF16),
            pltpu.VMEM((n * blk, width), BF16),
            pltpu.VMEM((relations * rows, n * blk), BF16),
            pltpu.VMEM((relations * rows, 128), F32),
            pltpu.VMEM((relations * rows, width), BF16),
            pltpu.VMEM((relations, 2, chips * chunk, rows), BF16),
            pltpu.VMEM((chips, relations, chunk, width), F32),
            pltpu.VMEM((n * blk, relations * rows), BF16),
            pltpu.VMEM((rows, width), F32),
            pltpu.VMEM((groups, half, 2 * share), BF16),
            pltpu.VMEM((groups, half, 2 * share), BF16),
            pltpu.VMEM((half, 2 * share), F32),
            pltpu.VMEM((half, 2 * share), F32),
            pltpu.VMEM((1, 2 * share), F32),
            pltpu.VMEM((groups, half, 2 * share), BF16),
            pltpu.VMEM((rows, width), BF16),
            pltpu.VMEM((relations * rows, width), BF16),
            pltpu.VMEM((n, blk, width), BF16),
            pltpu.VMEM((groups, n, quarter, width), BF16),
            pltpu.VMEM((n, quarter, width), BF16),
            pltpu.VMEM((n, quarter, width), BF16),
            pltpu.VMEM((chips, relations, chunk, width), BF16),
            pltpu.VMEM((chips, relations, chunk, width), BF16),
            pltpu.VMEM((chips, relations, chunk, width), BF16),
            pltpu.VMEM((chips, relations, chunk, width), BF16),
            pltpu.VMEM((chips, relations, chunk, width), BF16),
            pltpu.VMEM((chips, relations, chunk, width), BF16),
            dma((2,)), dma((2,)), dma((8,)), dma, dma,
            dma((n, 2)), dma((n, 2, 2)),
            dma((2,)), dma((2,)), dma((n,)), dma((chips,)),
            dma((chips, relations)), dma((chips, relations)),
        ],
        compiler_params=pltpu.CompilerParams(
            collective_id=0, has_side_effects=True, vmem_limit_bytes=60 << 20
        ),
        name="layer",
    )(
        source_blocks, tile_count, tile_slot,
        features.reshape(sections, groups, quarter, width), cotangent, bias,
        tile_values.reshape(relations, rows * slot_total, blk), weights,
    )
    results = (out, grad_w, grad_f)
    out, grad_w, grad_f = pl.pallas_call(
        hand_over,
        out_shape=tuple(jax.ShapeDtypeStruct(x.shape, x.dtype) for x in results),
        in_specs=[vmem] * 3,
        out_specs=(vmem,) * 3,
        name="hand_over",
    )(*results)
    return (out.T, grad_w, grad_f)


def solution(mesh):
    placed = (
        P("tgt", None),
        P("rel", None, None),
        P(),
        P("tgt", None),
        P("rel", "tgt", None, None),
        P("rel", "tgt"),
        P("rel", "tgt", None),
        P(),
    )
    return jax.shard_map(
        functools.partial(per_device, mesh.shape["tgt"], mesh.shape["rel"]),
        mesh=mesh,
        in_specs=placed,
        out_specs=(P("tgt", "rel"), P("rel", "tgt", None), P("tgt", "rel", None)),
        check_vma=False,
    )
```

time: 78.7 us -> 73.6 us (0.935)
  the two profiles are of different devices: /device:TPU:0 before, /device:TPU:1 now
where the time goes in v1:
time: 73.6 us; the launch traced here: 73.4 us
  Pallas kernels  72.8 us (99%)
    pallas_call x1, Pallas kernels, per_device(): pl.pallas_call(functools.partial(kernel, n, groups), out_shape=(jax.Shape...  70.7 us
    pallas_call x1, Pallas kernels, per_device(): pl.pallas_call(hand_over, out_shape=tuple((jax.ShapeDtypeStruct(x.shape,...  2.08 us

profile of v1, /device:TPU:1, one launch (start us, length us, event | category | flops | bytes accessed | tf_op | source)
XLA Modules:
  0.0 73.4 jit_solution(13394545629701322018)
XLA Ops:
  0.6 70.7 %layer.1 = (bf16[192,256]{1,0:T(8,128)(2,1)}, f32[2,96,768]{2,1,0:T(8,128)}, f32[2,32,768]{2,1,0:T(8,128)}) custom-call(s32[8,8]{1,0:T(8,128)} %table.1, s32[2,2]{1,0:T(2,128)} %counts.1, s32[2,2,8]{2,1,0:T(2,128)} %slots.1, bf16[2,4,32,768]{3,2,1,0:T(8,128)(2,1)} %bitcast.4, bf16[256,768]{1,0:T(8,128)(2,1)} %cot.1, f32[768]{0:T(1024)} %bias.1, ...), custom_call_target="tpu_custom_call" | custom-call | tf_op jit(solution)/shard_map/layer/pallas_call | solution.py:585
  71.3 2.1 %hand_over.1 = (bf16[192,256]{1,0:T(8,128)(2,1)}, f32[2,96,768]{2,1,0:T(8,128)}, f32[2,32,768]{2,1,0:T(8,128)}) custom-call(bf16[192,256]{1,0:T(8,128)(2,1)} %get-tuple-element.9.out_in, f32[2,96,768]{2,1,0:T(8,128)} %get-tuple-element.10.grad_w_in, f32[2,32,768]{2,1,0:T(8,128)} %get-tuple-element.11.grad_f_in), custom_call_target="tpu_custom_call" | custom-call | tf_op jit(solution)/shard_map/hand_over/pallas_call | solution.py:646

commit v2 on v1

--- a/solution.py
+++ b/solution.py
@@ -34,10 +34,9 @@
 def kernel(
     n, groups,
     table, counts, slots,
-    feat, cot, bias, values_hbm, weights_hbm,
-    out_hbm, grad_w_hbm, grad_f_hbm,
-    out, grad_w, grad_f, out_sem,
-    weights, values, gathered, partner_staged, masked, masked_t, fetched, adj, scale, msg, msg_t, wg_own, adj_t, pre,
+    feat_hbm, cot_hbm, bias, values_hbm, weights_hbm,
+    out, grad_w, grad_f,
+    weights, values, feat, cot, gathered, partner_staged, masked, masked_t, fetched, adj, scale, msg, msg_t, wg_own, adj_t, pre,
     pre_send, pre_recv, cot_own, active, bias_own, gp_all, gp, gm,
     part, part_recv, part_sum, part_back,
     wg_pair, wg_pair_recv, up_send, up_recv, down_send, down_recv,
@@ -82,8 +81,12 @@
 
     load_w = pltpu.make_async_copy(weights_hbm, weights, load_sem.at[0])
     load_v = pltpu.make_async_copy(values_hbm, values, load_sem.at[1])
+    load_f = pltpu.make_async_copy(feat_hbm, feat, load_sem.at[2])
+    load_c = pltpu.make_async_copy(cot_hbm, cot, load_sem.at[3])
+    load_f.start()
     load_v.start()
     load_w.start()
+    load_c.start()
 
     barrier = pltpu.get_barrier_semaphore()
 
@@ -100,8 +103,6 @@
             total = total + feat[k].reshape(blk, width).astype(F32) * is_one(table[t, me] == k)
         return total.astype(BF16)
 
-    fetched[aligned(me * blk, blk, blk), :] = whole_block(me)
-    partner_staged[...] = whole_block(partner)
     pl.semaphore_wait(barrier, n - 1 + groups - 1)
 
     cut = width // 2
@@ -136,16 +137,33 @@
         device_id=(grp, partner), device_id_type=MESH,
     )
 
+    def leap_rows(z, h):
+        return pltpu.make_async_remote_copy(
+            src_ref=feat_hbm.at[:, grp, :, columns(h)], dst_ref=gathered.at[me, :, :, columns(h)],
+            send_sem=sent_sem.at[0], recv_sem=a_recv.at[me, h],
+            device_id=(grp, z * 2 + core), device_id_type=MESH,
+        )
+
     for h in range(2):
         @pl.when(chip < chips - 1)
         def _():
-            climb_rows(me, h, feat.at[:, grp, :, columns(h)]).start()
+            climb_rows(me, h, feat_hbm.at[:, grp, :, columns(h)]).start()
 
         @pl.when(chip > 0)
         def _():
-            descend_rows(me, h, feat.at[:, grp, :, columns(h)]).start()
-
+            descend_rows(me, h, feat_hbm.at[:, grp, :, columns(h)]).start()
+
+    @pl.loop(0, chips)
+    def _(z):
+        @pl.when((z > chip + 2) | (z < chip - 2))
+        def _():
+            for h in range(2):
+                leap_rows(z, h).start()
+
+    load_f.wait()
+    partner_staged[...] = whole_block(partner)
     fetch_pair.start()
+    fetched[aligned(me * blk, blk, blk), :] = whole_block(me)
 
     sent = range(4) if square else range(groups - 1)
 
@@ -197,11 +215,11 @@
         o = near(2 * k)
         across_rows(o, h).wait_recv()
 
-        @pl.when((o < me) & (chip < chips - 1))
+        @pl.when((o // 2 == chip - 1) & (chip < chips - 1))
         def _():
             climb_rows(o, h, gathered.at[o, :, :, columns(h)]).start()
 
-        @pl.when((o > me) & (chip > 0))
+        @pl.when((o // 2 == chip + 1) & (chip > 0))
         def _():
             descend_rows(o, h, gathered.at[o, :, :, columns(h)]).start()
 
@@ -320,6 +338,7 @@
         for c in range(2):
             msg_t[r, c] = jnp.concatenate([sliced[z * 2 + c] for z in range(chips)], axis=0).astype(BF16)
 
+    load_c.wait()
     for k in range(groups):
         @pl.when(grp == k)
         def _():
@@ -353,11 +372,6 @@
     for h in range(2):
         out[:, h * (rows // 2) : (h + 1) * (rows // 2)] = upright[h * share : (h + 1) * share].astype(BF16)
 
-    save_out = pltpu.make_async_copy(out, out_hbm, out_sem.at[0])
-    save_w = pltpu.make_async_copy(grad_w, grad_w_hbm, out_sem.at[1])
-    save_f = pltpu.make_async_copy(grad_f, grad_f_hbm, out_sem.at[2])
-    save_out.start()
-
     for p in range(2):
         drain(pre_recv.at[1:groups, p * piece_rows : (p + 1) * piece_rows, :], g_recv.at[p])
     half = rows // 2
@@ -524,8 +538,6 @@
             descend(chip, r).wait_recv()
             grad_w[r] = grad_w[r] + down_recv[chip, r].astype(F32)
 
-    save_w.start()
-
     drain(part_sum.at[: n - 1], back_sem)
 
     for k in range(sections):
@@ -538,18 +550,15 @@
         for k in range(sections):
             grad_f[k] = grad_f[k] + addend * is_one(wanted == k)
 
-    save_f.start()
-
     fetch_pair.wait_send()
-    at_end = (chip == 0) | (chip == chips - 1)
-
-    @pl.when(at_end)
-    def _():
-        drain(gathered.at[:chips], sent_sem.at[0])
-
-    @pl.when(jnp.logical_not(at_end))
-    def _():
-        drain(gathered, sent_sem.at[0])
+    for z in range(chips):
+        near_by = (z > 0) + (z < chips - 1)
+        relayed = 2 * (0 < z < chips - 1)
+        far = sum(abs(y - z) > 2 for y in range(chips))
+
+        @pl.when(chip == z)
+        def _():
+            drain(gathered.at[: near_by + relayed + far + chips - 1], sent_sem.at[0])
 
     drain(fetched.at[: (n - 2) * (groups - 1) * quarter, :], sent_sem.at[1])
     drain(pre_recv.at[1:groups], sent_sem.at[2])
@@ -558,15 +567,14 @@
     drain(up_send.at[: chips - 1], sent_sem.at[5])
     drain(part_recv.at[1:groups], sent_sem.at[6])
     drain(part_sum.at[: n - 1], sent_sem.at[7])
-    save_out.wait()
-    save_w.wait()
-    save_f.wait()
-
-
-def hand_over(out_in, grad_w_in, grad_f_in, out, grad_w, grad_f):
-    out[...] = out_in[...]
-    grad_w[...] = grad_w_in[...]
-    grad_f[...] = grad_f_in[...]
+
+
+def hand_over(*refs):
+    copies = [pltpu.make_async_copy(refs[k], refs[3 + k], refs[6].at[k]) for k in range(3)]
+    for copy in copies:
+        copy.start()
+    for copy in copies:
+        copy.wait()
 
 
 def per_device(
@@ -581,23 +589,22 @@
     vmem = pl.BlockSpec(memory_space=pltpu.VMEM)
     smem = pl.BlockSpec(memory_space=pltpu.SMEM)
     anywhere = pl.BlockSpec(memory_space=pl.ANY)
+    hbm = pl.BlockSpec(memory_space=pltpu.HBM)
     dma = pltpu.SemaphoreType.DMA
     out, grad_w, grad_f = pl.pallas_call(
         functools.partial(kernel, n, groups),
         out_shape=(
-            jax.ShapeDtypeStruct((share, rows), BF16),
-            jax.ShapeDtypeStruct((relations, chunk, width), F32),
-            jax.ShapeDtypeStruct((sections, quarter, width), F32),
-        ),
-        in_specs=[smem, smem, smem, vmem, vmem, vmem, anywhere, anywhere],
-        out_specs=(anywhere, anywhere, anywhere),
-        scratch_shapes=[
             pltpu.VMEM((share, rows), BF16),
             pltpu.VMEM((relations, chunk, width), F32),
             pltpu.VMEM((sections, quarter, width), F32),
-            dma((3,)),
+        ),
+        in_specs=[smem, smem, smem, hbm, hbm, vmem, hbm, hbm],
+        out_specs=(vmem, vmem, vmem),
+        scratch_shapes=[
             pltpu.VMEM((relations, width, width), BF16),
             pltpu.VMEM((relations, rows * slot_total, blk), jnp.int32),
+            pltpu.VMEM((sections, groups, quarter, width), BF16),
+            pltpu.VMEM((rows, width), BF16),
             pltpu.VMEM((n, sections, quarter, width), BF16),
             pltpu.VMEM((blk, width), BF16),
             pltpu.VMEM((slot_total, blk, blk), BF16),
@@ -628,7 +635,7 @@
             pltpu.VMEM((chips, relations, chunk, width), BF16),
             pltpu.VMEM((chips, relations, chunk, width), BF16),
             pltpu.VMEM((chips, relations, chunk, width), BF16),
-            dma((2,)), dma((2,)), dma((8,)), dma, dma,
+            dma((4,)), dma((2,)), dma((8,)), dma, dma,
             dma((n, 2)), dma((n, 2, 2)),
             dma((2,)), dma((2,)), dma((n,)), dma((chips,)),
             dma((chips, relations)), dma((chips, relations)),
@@ -647,7 +654,9 @@
         hand_over,
         out_shape=tuple(jax.ShapeDtypeStruct(x.shape, x.dtype) for x in results),
         in_specs=[vmem] * 3,
-        out_specs=(vmem,) * 3,
+        out_specs=(anywhere,) * 3,
+        scratch_shapes=[dma((3,))],
+        compiler_params=pltpu.CompilerParams(vmem_limit_bytes=4 << 20),
         name="hand_over",
     )(*results)
     return (out.T, grad_w, grad_f)

time: 73.6 us -> 72.1 us (0.980)
  Pallas kernels: 72.8 us -> 71.3 us
    pallas_call x1, Pallas kernels: 2.08 us -> 0.93 us  [per_device(): pl.pallas_call(hand_over, out_shape=tuple((jax.ShapeDtypeStruct(x.shape,...]
where the time goes in v2:
time: 72.1 us; the launch traced here: 72 us
  Pallas kernels  71.3 us (99%)
    pallas_call x1, Pallas kernels, per_device(): pl.pallas_call(functools.partial(kernel, n, groups), out_shape=(pltpu.VME...  70.4 us

profile of v2, /device:TPU:1, one launch (start us, length us, event | category | flops | bytes accessed | tf_op | source)
XLA Modules:
  0.0 72.0 jit_solution(13369577270311745876)
XLA Ops:
  0.6 70.4 %layer.1 = (bf16[192,256]{1,0:T(8,128)(2,1)S(1)}, f32[2,96,768]{2,1,0:T(8,128)S(1)}, f32[2,32,768]{2,1,0:T(8,128)S(1)}) custom-call(s32[8,8]{1,0:T(8,128)} %table.1, s32[2,2]{1,0:T(2,128)} %counts.1, s32[2,2,8]{2,1,0:T(2,128)} %slots.1, bf16[2,4,32,768]{3,2,1,0:T(8,128)(2,1)} %bitcast.4, bf16[256,768]{1,0:T(8,128)(2,1)} %cot_hbm.1, f32[768]{0:T(1024)} %bias.1, ...), custom_call_target="tpu_custom_call" | custom-call | tf_op jit(solution)/shard_map/layer/pallas_call | solution.py:594
  71.0 0.9 %hand_over.1 = (bf16[192,256]{1,0:T(8,128)(2,1)}, f32[2,96,768]{2,1,0:T(8,128)}, f32[2,32,768]{2,1,0:T(8,128)}) custom-call(bf16[192,256]{1,0:T(8,128)(2,1)S(1)} %get-tuple-element.9.refs_0_, f32[2,96,768]{2,1,0:T(8,128)S(1)} %get-tuple-element.10.refs_1_, f32[2,32,768]{2,1,0:T(8,128)S(1)} %get-tuple-element.11.refs_2_), custom_call_target="tpu_custom_call" | custom-call | tf_op jit(solution)/shard_map/hand_over/pallas_call | solution.py:653

commit v3 on v2

--- a/solution.py
+++ b/solution.py
@@ -36,12 +36,11 @@
     table, counts, slots,
     feat_hbm, cot_hbm, bias, values_hbm, weights_hbm,
     out, grad_w, grad_f,
-    weights, values, feat, cot, gathered, partner_staged, masked, masked_t, fetched, adj, scale, msg, msg_t, wg_own, adj_t, pre,
-    pre_send, pre_recv, cot_own, active, bias_own, gp_all, gp, gm,
-    part, part_recv, part_sum, part_back,
-    wg_pair, wg_pair_recv, up_send, up_recv, down_send, down_recv,
-    load_sem, pair_sem, sent_sem, spread_sem, back_sem,
-    a_recv, b_recv, p_recv, g_recv, d_recv, w_recv, u_recv, v_recv,
+    weights, values, feat, cot, gathered, partner_staged, masked, masked_t, fetched, adj, scale, turned_scratch, msg, msg_t, msg_all, msg_end, end_sum, end_send, end_recv, adj_t, pre,
+    pre_send, pre_recv, cot_own, active, bias_own, gp_all, gp_full, gm,
+    part, part_recv, relay, relay_recv, part_sum, part_back,
+    load_sem, pair_sem, sent_sem, spread_sem, back_sem, end_sem, help_sem,
+    a_recv, b_recv, p_recv, g_recv, d_recv, r_recv, msg_sem, line_sem, other_sem, across_sem,
 ):
     me = lax.axis_index("tgt")
     grp = lax.axis_index("rel")
@@ -59,6 +58,12 @@
 
     below, above_me = chip, chips - 1 - chip
     both = jnp.minimum(below, above_me)
+    assisted = chips == 4 or chips > 5
+    last = chips - 1
+    is_end = (chip == 0) | (chip == last)
+    agent_low, agent_high = 2, last - 2
+    helped = jnp.where(chip == agent_low, 0, last)
+    is_agent = (chip == agent_low) | (chip == agent_high)
 
     def near(j):
         k = j // 2 - 1
@@ -296,12 +301,50 @@
     drain(fetched.at[: late * quarter, :], spread_sem)
 
     tile_width = 256
-
-    @pl.loop(0, width // tile_width)
-    def _(c):
-        at = aligned(c * tile_width, tile_width, tile_width)
-        acc = jnp.dot(adj[...], fetched[:, at], preferred_element_type=F32)
-        msg[:, at] = (acc * scale[:, 0:1]).astype(BF16)
+    chunk = width // n
+    for c in range(width // tile_width):
+        at = slice(c * tile_width, (c + 1) * tile_width)
+        acc = jnp.dot(adj[...], fetched[:, at], preferred_element_type=F32) * scale[:, 0:1]
+        msg[:, at] = acc.astype(BF16)
+        for r in range(relations):
+            turned_scratch[r, at, :] = acc[r * rows : (r + 1) * rows, :].T
+
+    for r in range(relations):
+        msg_t[:, r] = turned_scratch[r].reshape(n, chunk, rows).astype(BF16)
+
+    def send_messages(target, z, landing, semaphore):
+        return pltpu.make_async_remote_copy(
+            src_ref=msg_t.at[target], dst_ref=landing.at[me],
+            send_sem=sent_sem.at[4], recv_sem=semaphore,
+            device_id=(grp, z * 2 + lax.rem(target, 2)), device_id_type=MESH,
+        )
+
+    def start_messages(j):
+        target = near(j)
+        z = target // 2
+        if not assisted:
+            send_messages(target, z, msg_all, msg_sem).start()
+            return
+        away = ((z == 0) & (chip >= agent_low)) | ((z == last) & (chip <= agent_high))
+
+        @pl.when(jnp.logical_not(away))
+        def _():
+            send_messages(target, z, msg_all, msg_sem).start()
+
+        agent = jnp.where(z == 0, agent_low, agent_high)
+
+        @pl.when(away & jnp.logical_not((agent == chip) & (lax.rem(target, 2) == core)))
+        def _():
+            send_messages(target, agent, msg_end, end_sem).start()
+
+    @pl.loop(2, n)
+    def _(j):
+        start_messages(j)
+
+    send_messages(partner, chip, msg_all, msg_sem).start()
+    msg_all[me] = msg_t[me]
+    if assisted:
+        msg_end[me] = msg_t[helped * 2 + core]
 
     @pl.loop(0, width // tile_width)
     def _(c):
@@ -331,12 +374,6 @@
     for p in range(2):
         for i in range(1, groups):
             reduce_pre(i, p).start()
-
-    for r in range(relations):
-        turned = msg[r * rows : (r + 1) * rows, :].astype(F32).T
-        sliced = turned.reshape(n, width // n, rows)
-        for c in range(2):
-            msg_t[r, c] = jnp.concatenate([sliced[z * 2 + c] for z in range(chips)], axis=0).astype(BF16)
 
     load_c.wait()
     for k in range(groups):
@@ -376,35 +413,108 @@
         drain(pre_recv.at[1:groups, p * piece_rows : (p + 1) * piece_rows, :], g_recv.at[p])
     half = rows // 2
     for h in range(2):
-        gp[h * half : (h + 1) * half, :] = jnp.concatenate(
+        gp_full[me, h * half : (h + 1) * half, :] = jnp.concatenate(
             [gp_all[k][:, h * share : (h + 1) * share].astype(F32) for k in range(groups)], axis=1
         ).astype(BF16)
 
-    def weight_chunks(r, c):
-        product = jnp.dot(msg_t[r, c], gp[...], preferred_element_type=F32)
-        return product.reshape(chips, width // n, width)
-
-    def pair(z):
-        return pltpu.make_async_remote_copy(
-            src_ref=wg_pair.at[z], dst_ref=wg_pair_recv.at[z],
-            send_sem=sent_sem.at[4], recv_sem=w_recv.at[z],
+    if square:
+        span, mine, other = half, jnp.where(core == 0, column, row), jnp.where(core == 0, beside, above)
+    else:
+        span, mine, other = rows, 0, grp
+
+    def piece_of(o, part_of):
+        return gp_full.at[o, aligned(part_of * span, span, span), :]
+
+    def climb_gp(o):
+        return pltpu.make_async_remote_copy(
+            src_ref=piece_of(o, mine), dst_ref=piece_of(o, mine),
+            send_sem=sent_sem.at[5], recv_sem=line_sem.at[o // 2],
+            device_id=(grp, jnp.minimum(chip + 1, chips - 1) * 2 + core), device_id_type=MESH,
+        )
+
+    def descend_gp(o):
+        return pltpu.make_async_remote_copy(
+            src_ref=piece_of(o, mine), dst_ref=piece_of(o, mine),
+            send_sem=sent_sem.at[5], recv_sem=line_sem.at[o // 2],
+            device_id=(grp, jnp.maximum(chip - 1, 0) * 2 + core), device_id_type=MESH,
+        )
+
+    def exchange_gp(o):
+        return pltpu.make_async_remote_copy(
+            src_ref=piece_of(o, mine), dst_ref=piece_of(o, mine),
+            send_sem=sent_sem.at[8], recv_sem=other_sem.at[o // 2],
+            device_id=(other, me), device_id_type=MESH,
+        )
+
+    def across_gp(o, part_of):
+        return pltpu.make_async_remote_copy(
+            src_ref=piece_of(o, part_of), dst_ref=piece_of(o, part_of),
+            send_sem=sent_sem.at[9], recv_sem=across_sem.at[o // 2],
             device_id=(grp, partner), device_id_type=MESH,
         )
 
-    for r in range(relations):
-        wg_pair[:, r] = weight_chunks(r, 1 - core).astype(BF16)
-
-    upper = chip >= chips // 2
-
-    def order(i):
-        return jnp.where(upper, i, chips - 1 - i)
-
-    @pl.loop(0, chips)
-    def _(i):
-        pair(order(i)).start()
-
-    for r in range(relations):
-        wg_own[:, r] = weight_chunks(r, core)
+    @pl.when(chip < chips - 1)
+    def _():
+        climb_gp(me).start()
+
+    @pl.when(chip > 0)
+    def _():
+        descend_gp(me).start()
+
+    for h in range(rows // span):
+        across_gp(me, h).start()
+
+    def gp_arrives(k):
+        o = near(2 * k)
+        climb_gp(o).wait_recv()
+
+        @pl.when((o < me) & (chip < last - assisted))
+        def _():
+            climb_gp(o).start()
+
+        @pl.when((o > me) & (chip > 0 + assisted))
+        def _():
+            descend_gp(o).start()
+
+        if square:
+            exchange_gp(o).start()
+        across_gp(o, mine).start()
+
+    def gp_completes(k):
+        if square:
+            o = near(2 * k)
+            pltpu.make_async_remote_copy(
+                src_ref=piece_of(o, 1 - mine), dst_ref=piece_of(o, 1 - mine),
+                send_sem=sent_sem.at[8], recv_sem=other_sem.at[o // 2],
+                device_id=(other, me), device_id_type=MESH,
+            ).wait_recv()
+            across_gp(o, 1 - mine).start()
+
+    def gp_crossed(o):
+        drain(gp_full.at[o], across_sem.at[o // 2])
+
+    def weigh(o):
+        chunk = width // n
+        if chunk % 16 == 0:
+            product = jnp.dot(
+                msg_all[o].reshape(relations * chunk, rows), gp_full[o], preferred_element_type=F32
+            )
+            grad_w[...] = grad_w[...] + product.reshape(relations, chunk, width)
+        else:
+            for r in range(relations):
+                grad_w[r] = grad_w[r] + jnp.dot(msg_all[o, r], gp_full[o], preferred_element_type=F32)
+
+    def weigh_end(o):
+        for r in range(relations):
+            end_sum[r] = end_sum[r] + jnp.dot(msg_end[o, r], gp_full[o], preferred_element_type=F32)
+
+    grad_w[...] = jnp.zeros(grad_w.shape, F32)
+    end_sum[...] = jnp.zeros(end_sum.shape, F32)
+    help_end = pltpu.make_async_remote_copy(
+        src_ref=end_send, dst_ref=end_recv,
+        send_sem=sent_sem.at[11], recv_sem=help_sem,
+        device_id=(grp, helped * 2 + core), device_id_type=MESH,
+    )
 
     @pl.loop(0, width // tile_width)
     def _(c):
@@ -412,133 +522,210 @@
         for r in range(relations):
             rows_r = slice(r * rows, (r + 1) * rows)
             grads = lax.dot_general(
-                gp[...], weights[r, at, :],
+                gp_full[me], weights[r, at, :],
                 (((1,), (1,)), ((), ())), preferred_element_type=F32,
             )
             gm[rows_r, at] = (grads * scale[rows_r, 0:1]).astype(BF16)
 
-    def climb(d, r):
-        return pltpu.make_async_remote_copy(
-            src_ref=up_send.at[d, r], dst_ref=up_recv.at[d, r],
-            send_sem=sent_sem.at[5], recv_sem=u_recv.at[d, r],
-            device_id=(grp, jnp.minimum(chip + 1, chips - 1) * 2 + core), device_id_type=MESH,
-        )
-
-    def descend(d, r):
-        return pltpu.make_async_remote_copy(
-            src_ref=down_send.at[d, r], dst_ref=down_recv.at[d, r],
-            send_sem=sent_sem.at[5], recv_sem=v_recv.at[d, r],
-            device_id=(grp, jnp.maximum(chip - 1, 0) * 2 + core), device_id_type=MESH,
-        )
-
-    def chip_sum(r, z):
-        return wg_own[z, r] + wg_pair_recv[z, r].astype(F32)
-
-    @pl.loop(0, chips)
-    def _(i):
-        z = order(i)
-        pair(z).wait_recv()
-
-        @pl.when((chip == 0) & (z > 0))
-        def _():
-            for r in range(relations):
-                up_send[z, r] = chip_sum(r, z).astype(BF16)
-                climb(z, r).start()
-
-        @pl.when((chip == chips - 1) & (z < chips - 1))
-        def _():
-            for r in range(relations):
-                down_send[z, r] = chip_sum(r, z).astype(BF16)
-                descend(z, r).start()
-
-    pieces = (chips - 1) * relations
-
-    def line_piece(step):
-        up = step - (chip - 1)
-        d = chips - 1 - up // relations
-        r = lax.rem(up, relations)
-
-        @pl.when((chip > 0) & (up >= 0) & (up < pieces) & (d > chip))
-        def _():
-            climb(d, r).wait_recv()
-            up_send[d, r] = (chip_sum(r, d) + up_recv[d, r].astype(F32)).astype(BF16)
-            climb(d, r).start()
-
-        down = step - (chips - 2 - chip)
-        f = down // relations
-        g = lax.rem(down, relations)
-
-        @pl.when((chip < chips - 1) & (down >= 0) & (down < pieces) & (f < chip))
-        def _():
-            descend(f, g).wait_recv()
-            down_send[f, g] = (chip_sum(g, f) + down_recv[f, g].astype(F32)).astype(BF16)
-            descend(f, g).start()
+    lower, higher = slice(0, cut), slice(cut, width)
+
+    def far(j):
+        return near(n - j + 2 * lax.rem(j, 2))
 
     def reduce_part(o, i):
-        return pltpu.make_async_remote_copy(
-            src_ref=part.at[o, aligned(rel(i) * quarter, quarter, quarter), :],
-            dst_ref=part_recv.at[i, o],
+        if square:
+            source = part.at[o, :, 1 - column, :, lower] if i == 1 else part.at[o, 1 - row, :, :, higher]
+            target, peer = part_recv.at[o, i - 1], (beside, above)[i - 1]
+        else:
+            source, target, peer = part.at[o, rel(i)], part_recv.at[i, o], rel(i)
+        return pltpu.make_async_remote_copy(
+            src_ref=source, dst_ref=target,
             send_sem=sent_sem.at[6], recv_sem=d_recv.at[o],
-            device_id=(rel(i), me), device_id_type=MESH,
+            device_id=(peer, me), device_id_type=MESH,
+        )
+
+    def relay_part(o, w):
+        return pltpu.make_async_remote_copy(
+            src_ref=relay.at[o, w], dst_ref=relay_recv.at[o, w],
+            send_sem=sent_sem.at[10], recv_sem=r_recv.at[o],
+            device_id=((above, beside)[w], me), device_id_type=MESH,
         )
 
     @pl.loop(1, chips + 1)
     def _(e):
-        z = lax.rem(chip + e, chips)
+        z = jnp.where(e == chips, chip, near(jnp.maximum(n - 2 * e, 2)) // 2)
         product = jnp.dot(
             adj_t[aligned(z * 2 * blk, 2 * blk, blk), :], gm[...], preferred_element_type=F32
         )
         for v in range(2):
             o = z * 2 + v
-            part[o] = product[v * blk : (v + 1) * blk].astype(BF16)
-            for i in range(1, groups):
+            part[o] = product[v * blk : (v + 1) * blk].astype(BF16).reshape(part.shape[1:])
+            for i in range(1, 3 if square else groups):
                 reduce_part(o, i).start()
 
     def give_back(j):
         return pltpu.make_async_remote_copy(
-            src_ref=part_sum.at[tgt(j)], dst_ref=part_back.at[me],
+            src_ref=part_sum.at[far(j)], dst_ref=part_back.at[me],
             send_sem=sent_sem.at[7], recv_sem=back_sem,
-            device_id=(grp, tgt(j)), device_id_type=MESH,
-        )
+            device_id=(grp, far(j)), device_id_type=MESH,
+        )
+
+    def relayed(o):
+        if square:
+            drain(part_recv.at[o], d_recv.at[o])
+            up = part[o, 1 - row, column, :, lower].astype(F32) + part_recv[o, 0, 1 - row].astype(F32)
+            relay[o, 0] = up.astype(BF16)
+            relay_part(o, 0).start()
+            aside = part[o, row, 1 - column, :, higher].astype(F32) + part_recv[o, 1, 1 - column].astype(F32)
+            relay[o, 1] = aside.astype(BF16)
+            relay_part(o, 1).start()
 
     def reduced(o):
-        total = part[o, aligned(grp * quarter, quarter, quarter), :].astype(F32)
+        if square:
+            drain(relay_recv.at[o], r_recv.at[o])
+            first = part[o, row, column, :, lower].astype(F32) + part_recv[o, 0, row].astype(F32)
+            second = part[o, row, column, :, higher].astype(F32) + part_recv[o, 1, column].astype(F32)
+            first = first + relay_recv[o, 0].astype(F32)
+            second = second + relay_recv[o, 1].astype(F32)
+            return jnp.concatenate([first, second], axis=1).astype(BF16)
+        total = part[o, grp].astype(F32)
         drain(part_recv.at[1:groups, o], d_recv.at[o])
         for i in range(1, groups):
             total = total + part_recv[i, o].astype(F32)
         return total.astype(BF16)
 
     def send_reduced(j):
-        part_sum[tgt(j)] = reduced(tgt(j))
+        part_sum[far(j)] = reduced(far(j))
         give_back(j).start()
 
-    @pl.loop(0, pieces + chips - 2)
-    def _(step):
-        line_piece(step)
-
-        @pl.when(step + 2 < n)
-        def _():
-            send_reduced(step + 2)
-
-    send_reduced(1)
+    relays = both > 0
+    weigh(me)
+    gp_arrives(1)
+
+    @pl.when(relays)
+    def _():
+        gp_arrives(2)
+
+    @pl.loop(2, n - 2)
+    def _(j):
+        relayed(far(j))
+
+    if not assisted:
+        @pl.when(jnp.logical_not(relays))
+        def _():
+            gp_arrives(2)
+
+    relayed(far(n - 2))
+    relayed(far(n - 1))
+
+    @pl.when(relays)
+    def _():
+        @pl.loop(3, chips)
+        def _(k):
+            gp_arrives(k)
+
+    relayed(partner)
+    relayed(me)
+    sides = jnp.where(helped == 0, last - chip, chip)
+
+    def beyond(i):
+        return jnp.where(helped == 0, chip + 1, chip - 1 - (sides - 1)) + i
+
+    def complete(k):
+        gp_completes(k)
+        gp_crossed(near(2 * k + 1))
+
+    soon = chips == 4
+    if assisted and soon:
+        @pl.when(is_agent)
+        def _():
+            complete(1)
+            complete(2)
+            gp_crossed(partner)
+
+    def help_out():
+        drain(msg_end.at[: 2 * (chips - 2) - 1], end_sem)
+        weigh_end(me)
+        weigh_end(partner)
+
+        @pl.loop(0, sides)
+        def _(i):
+            weigh_end(beyond(i) * 2)
+            weigh_end(beyond(i) * 2 + 1)
+
+        end_send[...] = end_sum[...].astype(BF16)
+        help_end.start()
+
+    if assisted and soon:
+        pl.when(is_agent)(help_out)
+
+
+    @pl.loop(2, n)
+    def _(j):
+        send_reduced(j)
+
+    if not assisted:
+        @pl.when(jnp.logical_not(relays))
+        def _():
+            @pl.loop(3, chips)
+            def _(k):
+                gp_arrives(k)
+
+    part_sum[partner] = reduced(partner)
+    give_partner = pltpu.make_async_remote_copy(
+        src_ref=part_sum.at[partner], dst_ref=part_back.at[me],
+        send_sem=sent_sem.at[7], recv_sem=back_sem,
+        device_id=(grp, partner), device_id_type=MESH,
+    )
+    give_partner.start()
     part_back[me] = reduced(me)
 
-    for r in range(relations):
-        grad_w[r] = chip_sum(r, chip)
-
-    @pl.when(chip > 0)
-    def _():
-        for r in range(relations):
-            climb(chip, r).wait_recv()
-            grad_w[r] = grad_w[r] + up_recv[chip, r].astype(F32)
-
-    @pl.when(chip < chips - 1)
-    def _():
-        for r in range(relations):
-            descend(chip, r).wait_recv()
-            grad_w[r] = grad_w[r] + down_recv[chip, r].astype(F32)
+    if assisted:
+        @pl.when(is_end)
+        def _():
+            drain(msg_all.at[:3], msg_sem)
+
+        @pl.when(jnp.logical_not(is_end))
+        def _():
+            drain(msg_all.at[: n - 1], msg_sem)
+    else:
+        drain(msg_all.at[: n - 1], msg_sem)
+
+    reach = jnp.where(is_end, 2, chips) if assisted else chips
+    done = jnp.where(is_end, 1, 3) if assisted and soon else 1
+
+    @pl.loop(done, reach)
+    def _(k):
+        gp_completes(k)
+
+    @pl.loop(done, reach)
+    def _(k):
+        gp_crossed(near(2 * k + 1))
+
+    if assisted and soon:
+        @pl.when(is_end)
+        def _():
+            gp_crossed(partner)
+    else:
+        gp_crossed(partner)
+
+    weigh(partner)
+
+    @pl.loop(1, reach)
+    def _(k):
+        weigh(near(2 * k))
+        weigh(near(2 * k + 1))
+
+    if assisted and not soon:
+        pl.when(is_agent)(help_out)
 
     drain(part_sum.at[: n - 1], back_sem)
+    if assisted:
+        @pl.when(is_end)
+        def _():
+            help_end.wait_recv()
+            grad_w[...] = grad_w[...] + end_recv[...].astype(F32)
+
 
     for k in range(sections):
         grad_f[k] = jnp.zeros((quarter, width), F32)
@@ -563,9 +750,41 @@
     drain(fetched.at[: (n - 2) * (groups - 1) * quarter, :], sent_sem.at[1])
     drain(pre_recv.at[1:groups], sent_sem.at[2])
     drain(pre_recv.at[1:groups], sent_sem.at[3])
-    drain(wg_pair, sent_sem.at[4])
-    drain(up_send.at[: chips - 1], sent_sem.at[5])
-    drain(part_recv.at[1:groups], sent_sem.at[6])
+    if assisted:
+        @pl.when(is_agent)
+        def _():
+            drain(msg_all.at[: n - 2], sent_sem.at[4])
+            help_end.wait_send()
+
+        @pl.when(jnp.logical_not(is_agent))
+        def _():
+            drain(msg_all.at[: n - 1], sent_sem.at[4])
+    else:
+        drain(msg_all.at[: n - 1], sent_sem.at[4])
+
+    for z in range(chips):
+        at_end = z in (0, last)
+        climbs = z * (z + 1 <= last - assisted) + (z < last)
+        descents = (last - z) * (z - 1 >= 0 + assisted) + (z > 0)
+        climbs, descents = (climbs if z < last else 0), (descents if z > 0 else 0)
+        if at_end:
+            climbs, descents = int(z == 0), int(z == last)
+        known = 1 if at_end and assisted else last
+
+        @pl.when(chip == z)
+        def _():
+            if square:
+                drain(fetched.at[: (climbs + descents) * span, :], sent_sem.at[5])
+                drain(fetched.at[: known * span, :], sent_sem.at[8])
+            else:
+                drain(gp_full.at[: climbs + descents], sent_sem.at[5])
+            drain(gp_full.at[: known + 1], sent_sem.at[9])
+
+    if square:
+        drain(part_recv, sent_sem.at[6])
+        drain(relay_recv, sent_sem.at[10])
+    else:
+        drain(part_recv.at[1:groups], sent_sem.at[6])
     drain(part_sum.at[: n - 1], sent_sem.at[7])
 
 
@@ -586,6 +805,8 @@
     sections = rows // blk
     quarter, share, chunk, chips = blk // groups, width // groups, width // n, n // 2
     half = rows // 2
+    square = groups == 4
+    grid = (2, 2) if square else (groups,)
     vmem = pl.BlockSpec(memory_space=pltpu.VMEM)
     smem = pl.BlockSpec(memory_space=pltpu.SMEM)
     anywhere = pl.BlockSpec(memory_space=pl.ANY)
@@ -612,9 +833,14 @@
             pltpu.VMEM((n * blk, width), BF16),
             pltpu.VMEM((relations * rows, n * blk), BF16),
             pltpu.VMEM((relations * rows, 128), F32),
+            pltpu.VMEM((relations, width, rows), F32),
             pltpu.VMEM((relations * rows, width), BF16),
-            pltpu.VMEM((relations, 2, chips * chunk, rows), BF16),
-            pltpu.VMEM((chips, relations, chunk, width), F32),
+            pltpu.VMEM((n, relations, chunk, rows), BF16),
+            pltpu.VMEM((n, relations, chunk, rows), BF16),
+            pltpu.VMEM((n, relations, chunk, rows), BF16),
+            pltpu.VMEM((relations, chunk, width), F32),
+            pltpu.VMEM((relations, chunk, width), BF16),
+            pltpu.VMEM((relations, chunk, width), BF16),
             pltpu.VMEM((n * blk, relations * rows), BF16),
             pltpu.VMEM((rows, width), F32),
             pltpu.VMEM((groups, half, 2 * share), BF16),
@@ -623,22 +849,18 @@
             pltpu.VMEM((half, 2 * share), F32),
             pltpu.VMEM((1, 2 * share), F32),
             pltpu.VMEM((groups, half, 2 * share), BF16),
-            pltpu.VMEM((rows, width), BF16),
+            pltpu.VMEM((n, rows, width), BF16),
             pltpu.VMEM((relations * rows, width), BF16),
-            pltpu.VMEM((n, blk, width), BF16),
-            pltpu.VMEM((groups, n, quarter, width), BF16),
+            pltpu.VMEM((n, *grid, quarter, width), BF16),
+            pltpu.VMEM((n, 2, 2, quarter, width // 2) if square else (groups, n, quarter, width), BF16),
+            pltpu.VMEM((n, 2, quarter, width // 2), BF16),
+            pltpu.VMEM((n, 2, quarter, width // 2), BF16),
             pltpu.VMEM((n, quarter, width), BF16),
             pltpu.VMEM((n, quarter, width), BF16),
-            pltpu.VMEM((chips, relations, chunk, width), BF16),
-            pltpu.VMEM((chips, relations, chunk, width), BF16),
-            pltpu.VMEM((chips, relations, chunk, width), BF16),
-            pltpu.VMEM((chips, relations, chunk, width), BF16),
-            pltpu.VMEM((chips, relations, chunk, width), BF16),
-            pltpu.VMEM((chips, relations, chunk, width), BF16),
-            dma((4,)), dma((2,)), dma((8,)), dma, dma,
+            dma((4,)), dma((2,)), dma((12,)), dma, dma, dma, dma,
             dma((n, 2)), dma((n, 2, 2)),
-            dma((2,)), dma((2,)), dma((n,)), dma((chips,)),
-            dma((chips, relations)), dma((chips, relations)),
+            dma((2,)), dma((2,)), dma((n,)), dma((n,)), dma,
+            dma((chips,)), dma((chips,)), dma((chips,)),
         ],
         compiler_params=pltpu.CompilerParams(
             collective_id=0, has_side_effects=True, vmem_limit_bytes=60 << 20

time: 72.1 us -> 70.3 us (0.975)
  Pallas kernels: 71.3 us -> 69 us
    pallas_call x1, Pallas kernels: 70.4 us -> 68.1 us  [per_device(): pl.pallas_call(functools.partial(kernel, n, groups), out_shape=(pltpu.VME...]
where the time goes in v3:
time: 70.3 us; the launch traced here: 69.7 us
  Pallas kernels  69 us (98%)
    pallas_call x1, Pallas kernels, per_device(): pl.pallas_call(functools.partial(kernel, n, groups), out_shape=(pltpu.VME...  68.1 us

profile of v3, /device:TPU:1, one launch (start us, length us, event | category | flops | bytes accessed | tf_op | source)
XLA Modules:
  0.0 69.7 jit_solution(6917590800122564815)
XLA Ops:
  0.6 68.1 %layer.1 = (bf16[192,256]{1,0:T(8,128)(2,1)S(1)}, f32[2,96,768]{2,1,0:T(8,128)S(1)}, f32[2,32,768]{2,1,0:T(8,128)S(1)}) custom-call(s32[8,8]{1,0:T(8,128)} %table.1, s32[2,2]{1,0:T(2,128)} %counts.1, s32[2,2,8]{2,1,0:T(2,128)} %slots.1, bf16[2,4,32,768]{3,2,1,0:T(8,128)(2,1)} %bitcast.4, bf16[256,768]{1,0:T(8,128)(2,1)} %cot_hbm.1, f32[768]{0:T(1024)} %bias.1, ...), custom_call_target="tpu_custom_call" | custom-call | tf_op jit(solution)/shard_map/layer/pallas_call | solution.py:815
  68.7 0.9 %hand_over.1 = (bf16[192,256]{1,0:T(8,128)(2,1)}, f32[2,96,768]{2,1,0:T(8,128)}, f32[2,32,768]{2,1,0:T(8,128)}) custom-call(bf16[192,256]{1,0:T(8,128)(2,1)S(1)} %get-tuple-element.9.refs_0_, f32[2,96,768]{2,1,0:T(8,128)S(1)} %get-tuple-element.10.refs_1_, f32[2,32,768]{2,1,0:T(8,128)S(1)} %get-tuple-element.11.refs_2_), custom_call_target="tpu_custom_call" | custom-call | tf_op jit(solution)/shard_map/hand_over/pallas_call | solution.py:875

commit v4 on v3

--- a/solution.py
+++ b/solution.py
@@ -38,8 +38,8 @@
     out, grad_w, grad_f,
     weights, values, feat, cot, gathered, partner_staged, masked, masked_t, fetched, adj, scale, turned_scratch, msg, msg_t, msg_all, msg_end, end_sum, end_send, end_recv, adj_t, pre,
     pre_send, pre_recv, cot_own, active, bias_own, gp_all, gp_full, gm,
-    part, part_recv, relay, relay_recv, part_sum, part_back,
-    load_sem, pair_sem, sent_sem, spread_sem, back_sem, end_sem, help_sem,
+    part, part_recv, relay, relay_recv, part_sum, part_back, inbox, crossed, gathered_sum, collected,
+    load_sem, pair_sem, sent_sem, spread_sem, back_sem, end_sem, help_sem, inbox_sem, crossed_sem, collect_sem,
     a_recv, b_recv, p_recv, g_recv, d_recv, r_recv, msg_sem, line_sem, other_sem, across_sem,
 ):
     me = lax.axis_index("tgt")
@@ -461,6 +461,21 @@
     def _():
         descend_gp(me).start()
 
+    whole_end = assisted and square
+    next_in = jnp.where(chip == 0, 1, last - 1)
+
+    def beside_end(o):
+        return ((o // 2 == 0) & (chip == 1)) | ((o // 2 == last) & (chip == last - 1))
+
+    if whole_end:
+        @pl.when(is_end)
+        def _():
+            pltpu.make_async_remote_copy(
+                src_ref=piece_of(me, 1 - mine), dst_ref=piece_of(me, 1 - mine),
+                send_sem=sent_sem.at[5], recv_sem=other_sem.at[chip],
+                device_id=(grp, next_in * 2 + core), device_id_type=MESH,
+            ).start()
+
     for h in range(rows // span):
         across_gp(me, h).start()
 
@@ -476,7 +491,11 @@
         def _():
             descend_gp(o).start()
 
-        if square:
+        if whole_end:
+            @pl.when(jnp.logical_not(beside_end(o)))
+            def _():
+                exchange_gp(o).start()
+        elif square:
             exchange_gp(o).start()
         across_gp(o, mine).start()
 
@@ -563,12 +582,71 @@
             for i in range(1, 3 if square else groups):
                 reduce_part(o, i).start()
 
+    far_chips = chips - 2
+    is_inner = (chip == 1) | (chip == last - 1)
+    low_side = chip <= 1
+
+    def crosses(o, source):
+        return ((source <= 1) & (o // 2 >= 2)) | ((source >= last - 1) & (o // 2 <= last - 2))
+
+    def hand(o, device, landing, semaphore):
+        return pltpu.make_async_remote_copy(
+            src_ref=part_sum.at[o], dst_ref=landing,
+            send_sem=sent_sem.at[7], recv_sem=semaphore,
+            device_id=(grp, device), device_id_type=MESH,
+        )
+
     def give_back(j):
-        return pltpu.make_async_remote_copy(
-            src_ref=part_sum.at[far(j)], dst_ref=part_back.at[me],
-            send_sem=sent_sem.at[7], recv_sem=back_sem,
-            device_id=(grp, far(j)), device_id_type=MESH,
-        )
+        o = far(j)
+        if not assisted:
+            hand(o, o, part_back.at[me], back_sem).start()
+            return
+        slot = jnp.where(low_side, jnp.maximum(o // 2 - 2, 0), jnp.minimum(o // 2, far_chips - 1))
+        odd = lax.rem(o, 2)
+        over = crosses(o, chip)
+
+        @pl.when(over & is_end)
+        def _():
+            hand(o, next_in * 2 + odd, inbox.at[core, slot], inbox_sem).start()
+
+        @pl.when(over & is_inner & (odd != core))
+        def _():
+            hand(o, partner, crossed.at[slot], crossed_sem).start()
+
+        @pl.when(jnp.logical_not(over & (is_end | is_inner)))
+        def _():
+            hand(o, o, part_back.at[me], back_sem).start()
+
+    def collect(slot):
+        z = jnp.where(low_side, slot + 2, slot)
+        side = jnp.where(low_side, 0, 1)
+        return pltpu.make_async_remote_copy(
+            src_ref=gathered_sum.at[slot], dst_ref=collected.at[side],
+            send_sem=sent_sem.at[12], recv_sem=collect_sem.at[side],
+            device_id=(grp, z * 2 + core), device_id_type=MESH,
+        )
+
+    def sum_for_far_side():
+        drain(crossed, crossed_sem)
+        drain(inbox, inbox_sem)
+        outer = jnp.where(low_side, 0, last)
+
+        @pl.loop(0, far_chips)
+        def _(slot):
+            o = jnp.where(low_side, slot + 2, slot) * 2 + core
+            terms = (
+                (me, part_sum[o].astype(F32)),
+                (partner, crossed[slot].astype(F32)),
+                (outer * 2, inbox[0, slot].astype(F32)),
+                (outer * 2 + 1, inbox[1, slot].astype(F32)),
+            )
+            for k in range(sections):
+                total = None
+                for t, term in terms:
+                    kept = term * is_one(table[t, o] == k)
+                    total = kept if total is None else total + kept
+                gathered_sum[slot, k] = total.astype(BF16)
+            collect(slot).start()
 
     def relayed(o):
         if square:
@@ -596,7 +674,7 @@
 
     def send_reduced(j):
         part_sum[far(j)] = reduced(far(j))
-        give_back(j).start()
+        give_back(j)
 
     relays = both > 0
     weigh(me)
@@ -609,6 +687,39 @@
     @pl.loop(2, n - 2)
     def _(j):
         relayed(far(j))
+
+    sides = jnp.where(helped == 0, last - chip, chip)
+
+    def beyond(i):
+        return jnp.where(helped == 0, chip + 1, chip - 1 - (sides - 1)) + i
+
+    def complete(k):
+        gp_completes(k)
+        gp_crossed(near(2 * k + 1))
+
+    soon = chips == 4
+    outward = jnp.where(chip == 1, 2, 1)
+    if assisted and soon:
+        @pl.when(is_agent)
+        def _():
+            complete(outward)
+            gp_crossed(partner)
+
+    def help_out():
+        drain(msg_end.at[: 2 * (chips - 2) - 1], end_sem)
+        weigh_end(me)
+        weigh_end(partner)
+
+        @pl.loop(0, sides)
+        def _(i):
+            weigh_end(beyond(i) * 2)
+            weigh_end(beyond(i) * 2 + 1)
+
+        end_send[...] = end_sum[...].astype(BF16)
+        help_end.start()
+
+    if assisted and soon:
+        pl.when(is_agent)(help_out)
 
     if not assisted:
         @pl.when(jnp.logical_not(relays))
@@ -626,39 +737,6 @@
 
     relayed(partner)
     relayed(me)
-    sides = jnp.where(helped == 0, last - chip, chip)
-
-    def beyond(i):
-        return jnp.where(helped == 0, chip + 1, chip - 1 - (sides - 1)) + i
-
-    def complete(k):
-        gp_completes(k)
-        gp_crossed(near(2 * k + 1))
-
-    soon = chips == 4
-    if assisted and soon:
-        @pl.when(is_agent)
-        def _():
-            complete(1)
-            complete(2)
-            gp_crossed(partner)
-
-    def help_out():
-        drain(msg_end.at[: 2 * (chips - 2) - 1], end_sem)
-        weigh_end(me)
-        weigh_end(partner)
-
-        @pl.loop(0, sides)
-        def _(i):
-            weigh_end(beyond(i) * 2)
-            weigh_end(beyond(i) * 2 + 1)
-
-        end_send[...] = end_sum[...].astype(BF16)
-        help_end.start()
-
-    if assisted and soon:
-        pl.when(is_agent)(help_out)
-
 
     @pl.loop(2, n)
     def _(j):
@@ -679,6 +757,8 @@
     )
     give_partner.start()
     part_back[me] = reduced(me)
+    if assisted:
+        pl.when(is_inner)(sum_for_far_side)
 
     if assisted:
         @pl.when(is_end)
@@ -692,15 +772,19 @@
         drain(msg_all.at[: n - 1], msg_sem)
 
     reach = jnp.where(is_end, 2, chips) if assisted else chips
-    done = jnp.where(is_end, 1, 3) if assisted and soon else 1
-
-    @pl.loop(done, reach)
+    waited = jnp.where(is_agent, outward, 0) if assisted and soon else 0
+
+    @pl.loop(1, reach)
     def _(k):
-        gp_completes(k)
-
-    @pl.loop(done, reach)
+        @pl.when(k != waited)
+        def _():
+            gp_completes(k)
+
+    @pl.loop(1, reach)
     def _(k):
-        gp_crossed(near(2 * k + 1))
+        @pl.when(k != waited)
+        def _():
+            gp_crossed(near(2 * k + 1))
 
     if assisted and soon:
         @pl.when(is_end)
@@ -719,23 +803,43 @@
     if assisted and not soon:
         pl.when(is_agent)(help_out)
 
-    drain(part_sum.at[: n - 1], back_sem)
+    for k in range(sections):
+        grad_f[k] = jnp.zeros((quarter, width), F32)
+
     if assisted:
+        for z in range(chips):
+            direct = n - 1 - 4 * (z >= 2) - 4 * (z <= last - 2)
+
+            @pl.when(chip == z)
+            def _():
+                drain(part_sum.at[:direct], back_sem)
+    else:
+        drain(part_sum.at[: n - 1], back_sem)
+
+    @pl.loop(0, n)
+    def _(t):
+        def add():
+            wanted = table[t, me]
+            addend = part_back[t].astype(F32)
+            for k in range(sections):
+                grad_f[k] = grad_f[k] + addend * is_one(wanted == k)
+
+        if assisted:
+            pl.when(jnp.logical_not(crosses(me, t // 2)))(add)
+        else:
+            add()
+
+    if assisted:
+        for side, has in ((0, chip >= 2), (1, chip <= last - 2)):
+            @pl.when(has)
+            def _():
+                drain(collected.at[side], collect_sem.at[side])
+                grad_f[...] = grad_f[...] + collected[side].astype(F32)
+
         @pl.when(is_end)
         def _():
             help_end.wait_recv()
             grad_w[...] = grad_w[...] + end_recv[...].astype(F32)
-
-
-    for k in range(sections):
-        grad_f[k] = jnp.zeros((quarter, width), F32)
-
-    @pl.loop(0, n)
-    def _(t):
-        wanted = table[t, me]
-        addend = part_back[t].astype(F32)
-        for k in range(sections):
-            grad_f[k] = grad_f[k] + addend * is_one(wanted == k)
 
     fetch_pair.wait_send()
     for z in range(chips):
@@ -770,12 +874,14 @@
         if at_end:
             climbs, descents = int(z == 0), int(z == last)
         known = 1 if at_end and assisted else last
+        doubled = int(at_end and assisted and square)
+        swapped = known - (assisted and z in (1, last - 1))
 
         @pl.when(chip == z)
         def _():
             if square:
-                drain(fetched.at[: (climbs + descents) * span, :], sent_sem.at[5])
-                drain(fetched.at[: known * span, :], sent_sem.at[8])
+                drain(fetched.at[: (climbs + descents + doubled) * span, :], sent_sem.at[5])
+                drain(fetched.at[: swapped * span, :], sent_sem.at[8])
             else:
                 drain(gp_full.at[: climbs + descents], sent_sem.at[5])
             drain(gp_full.at[: known + 1], sent_sem.at[9])
@@ -785,7 +891,17 @@
         drain(relay_recv, sent_sem.at[10])
     else:
         drain(part_recv.at[1:groups], sent_sem.at[6])
-    drain(part_sum.at[: n - 1], sent_sem.at[7])
+    if assisted:
+        @pl.when(is_inner)
+        def _():
+            drain(part_sum.at[: n - 1 - far_chips], sent_sem.at[7])
+            drain(gathered_sum, sent_sem.at[12])
+
+        @pl.when(jnp.logical_not(is_inner))
+        def _():
+            drain(part_sum.at[: n - 1], sent_sem.at[7])
+    else:
+        drain(part_sum.at[: n - 1], sent_sem.at[7])
 
 
 def hand_over(*refs):
@@ -857,7 +973,11 @@
             pltpu.VMEM((n, 2, quarter, width // 2), BF16),
             pltpu.VMEM((n, quarter, width), BF16),
             pltpu.VMEM((n, quarter, width), BF16),
-            dma((4,)), dma((2,)), dma((12,)), dma, dma, dma, dma,
+            pltpu.VMEM((2, chips - 2, quarter, width), BF16),
+            pltpu.VMEM((chips - 2, quarter, width), BF16),
+            pltpu.VMEM((chips - 2, sections, quarter, width), BF16),
+            pltpu.VMEM((2, sections, quarter, width), BF16),
+            dma((4,)), dma((2,)), dma((13,)), dma, dma, dma, dma, dma, dma, dma((2,)),
             dma((n, 2)), dma((n, 2, 2)),
             dma((2,)), dma((2,)), dma((n,)), dma((n,)), dma,
             dma((chips,)), dma((chips,)), dma((chips,)),

time: 70.3 us -> 65.3 us (0.929)
  Pallas kernels: 69 us -> 64.1 us
    pallas_call x1, Pallas kernels: 68.1 us -> 63.2 us  [per_device(): pl.pallas_call(functools.partial(kernel, n, groups), out_shape=(pltpu.VME...]
where the time goes in v4:
time: 65.3 us; the launch traced here: 64.8 us
  Pallas kernels  64.1 us (98%)
    pallas_call x1, Pallas kernels, per_device(): pl.pallas_call(functools.partial(kernel, n, groups), out_shape=(pltpu.VME...  63.2 us

profile of v4, /device:TPU:1, one launch (start us, length us, event | category | flops | bytes accessed | tf_op | source)
XLA Modules:
  0.0 64.8 jit_solution(12517779738372760530)
XLA Ops:
  0.6 63.2 %layer.1 = (bf16[192,256]{1,0:T(8,128)(2,1)S(1)}, f32[2,96,768]{2,1,0:T(8,128)S(1)}, f32[2,32,768]{2,1,0:T(8,128)S(1)}) custom-call(s32[8,8]{1,0:T(8,128)} %table.1, s32[2,2]{1,0:T(2,128)} %counts.1, s32[2,2,8]{2,1,0:T(2,128)} %slots.1, bf16[2,4,32,768]{3,2,1,0:T(8,128)(2,1)} %bitcast.4, bf16[256,768]{1,0:T(8,128)(2,1)} %cot_hbm.1, f32[768]{0:T(1024)} %bias.1, ...), custom_call_target="tpu_custom_call" | custom-call | tf_op jit(solution)/shard_map/layer/pallas_call | solution.py:931
  63.8 0.9 %hand_over.1 = (bf16[192,256]{1,0:T(8,128)(2,1)}, f32[2,96,768]{2,1,0:T(8,128)}, f32[2,32,768]{2,1,0:T(8,128)}) custom-call(bf16[192,256]{1,0:T(8,128)(2,1)S(1)} %get-tuple-element.9.refs_0_, f32[2,96,768]{2,1,0:T(8,128)S(1)} %get-tuple-element.10.refs_1_, f32[2,32,768]{2,1,0:T(8,128)S(1)} %get-tuple-element.11.refs_2_), custom_call_target="tpu_custom_call" | custom-call | tf_op jit(solution)/shard_map/hand_over/pallas_call | solution.py:995

commit v5 on v4

--- a/solution.py
+++ b/solution.py
@@ -39,7 +39,7 @@
     weights, values, feat, cot, gathered, partner_staged, masked, masked_t, fetched, adj, scale, turned_scratch, msg, msg_t, msg_all, msg_end, end_sum, end_send, end_recv, adj_t, pre,
     pre_send, pre_recv, cot_own, active, bias_own, gp_all, gp_full, gm,
     part, part_recv, relay, relay_recv, part_sum, part_back, inbox, crossed, gathered_sum, collected,
-    load_sem, pair_sem, sent_sem, spread_sem, back_sem, end_sem, help_sem, inbox_sem, crossed_sem, collect_sem,
+    load_sem, pair_sem, sent_sem, spread_sem, back_sem, end_sem, help_sem, inbox_sem, crossed_sem, collect_sem, slab_sem, cross_slab_sem,
     a_recv, b_recv, p_recv, g_recv, d_recv, r_recv, msg_sem, line_sem, other_sem, across_sem,
 ):
     me = lax.axis_index("tgt")
@@ -62,6 +62,10 @@
     last = chips - 1
     is_end = (chip == 0) | (chip == last)
     agent_low, agent_high = 2, last - 2
+    soon = chips == 4
+    sliced = soon and groups == 4
+    outward = jnp.where(chip == 1, 2, 1)
+    outer_chip = jnp.where(chip == 1, 0, last)
     helped = jnp.where(chip == agent_low, 0, last)
     is_agent = (chip == agent_low) | (chip == agent_high)
 
@@ -337,9 +341,15 @@
         def _():
             send_messages(target, agent, msg_end, end_sem).start()
 
-    @pl.loop(2, n)
+    @pl.loop(4, n)
     def _(j):
-        start_messages(j)
+        start_messages(n + 3 - j)
+
+    def start_next_messages():
+        start_messages(2)
+        start_messages(3)
+
+    pl.when(jnp.logical_not(is_end))(start_next_messages)
 
     send_messages(partner, chip, msg_all, msg_sem).start()
     msg_all[me] = msg_t[me]
@@ -361,7 +371,8 @@
     for k in range(groups):
         pre_send[k] = pack(whole, k * share, share).astype(BF16)
 
-    piece_rows = rows // 4
+    pieces = 4
+    piece_rows = rows // 2 // pieces
 
     def reduce_pre(i, p):
         at = slice(p * piece_rows, (p + 1) * piece_rows)
@@ -371,7 +382,7 @@
             device_id=(rel(i), me), device_id_type=MESH,
         )
 
-    for p in range(2):
+    for p in range(pieces):
         for i in range(1, groups):
             reduce_pre(i, p).start()
 
@@ -391,7 +402,7 @@
             device_id=(rel(i), me), device_id_type=MESH,
         )
 
-    for p in range(2):
+    for p in range(pieces):
         at = slice(p * piece_rows, (p + 1) * piece_rows)
         total = pre_send[grp, at, :].astype(F32)
         drain(pre_recv.at[1:groups, at, :], p_recv.at[p])
@@ -409,13 +420,14 @@
     for h in range(2):
         out[:, h * (rows // 2) : (h + 1) * (rows // 2)] = upright[h * share : (h + 1) * share].astype(BF16)
 
-    for p in range(2):
-        drain(pre_recv.at[1:groups, p * piece_rows : (p + 1) * piece_rows, :], g_recv.at[p])
     half = rows // 2
-    for h in range(2):
-        gp_full[me, h * half : (h + 1) * half, :] = jnp.concatenate(
-            [gp_all[k][:, h * share : (h + 1) * share].astype(F32) for k in range(groups)], axis=1
-        ).astype(BF16)
+    for p in range(pieces):
+        at = slice(p * piece_rows, (p + 1) * piece_rows)
+        drain(pre_recv.at[1:groups, at, :], g_recv.at[p])
+        for h in range(2):
+            gp_full[me, h * half + p * piece_rows : h * half + (p + 1) * piece_rows, :] = jnp.concatenate(
+                [gp_all[k, at, h * share : (h + 1) * share].astype(F32) for k in range(groups)], axis=1
+            ).astype(BF16)
 
     if square:
         span, mine, other = half, jnp.where(core == 0, column, row), jnp.where(core == 0, beside, above)
@@ -453,21 +465,42 @@
             device_id=(grp, partner), device_id_type=MESH,
         )
 
-    @pl.when(chip < chips - 1)
+    whole_end = assisted and square
+    next_in = jnp.where(chip == 0, 1, last - 1)
+
+    def slab(o, c):
+        return gp_full.at[o, :, columns(c)]
+
+    def across_slab(o, c):
+        return pltpu.make_async_remote_copy(
+            src_ref=slab(o, c), dst_ref=slab(o, c),
+            send_sem=sent_sem.at[9], recv_sem=cross_slab_sem.at[c],
+            device_id=(grp, partner), device_id_type=MESH,
+        )
+
+    def beside_end(o):
+        return ((o // 2 == 0) & (chip == 1)) | ((o // 2 == last) & (chip == last - 1))
+
+    along = jnp.logical_not(is_end) if sliced else chip >= 0
+
+    @pl.when(along & (chip < chips - 1))
     def _():
         climb_gp(me).start()
 
-    @pl.when(chip > 0)
+    @pl.when(along & (chip > 0))
     def _():
         descend_gp(me).start()
 
-    whole_end = assisted and square
-    next_in = jnp.where(chip == 0, 1, last - 1)
-
-    def beside_end(o):
-        return ((o // 2 == 0) & (chip == 1)) | ((o // 2 == last) & (chip == last - 1))
-
-    if whole_end:
+    if sliced:
+        @pl.when(is_end)
+        def _():
+            for c in range(2):
+                pltpu.make_async_remote_copy(
+                    src_ref=slab(me, c), dst_ref=slab(me, c),
+                    send_sem=sent_sem.at[5], recv_sem=slab_sem.at[c],
+                    device_id=(grp, next_in * 2 + core), device_id_type=MESH,
+                ).start()
+    elif whole_end:
         @pl.when(is_end)
         def _():
             pltpu.make_async_remote_copy(
@@ -478,6 +511,7 @@
 
     for h in range(rows // span):
         across_gp(me, h).start()
+
 
     def gp_arrives(k):
         o = near(2 * k)
@@ -570,9 +604,7 @@
             device_id=((above, beside)[w], me), device_id_type=MESH,
         )
 
-    @pl.loop(1, chips + 1)
-    def _(e):
-        z = jnp.where(e == chips, chip, near(jnp.maximum(n - 2 * e, 2)) // 2)
+    def start_parts(z):
         product = jnp.dot(
             adj_t[aligned(z * 2 * blk, 2 * blk, blk), :], gm[...], preferred_element_type=F32
         )
@@ -581,6 +613,10 @@
             part[o] = product[v * blk : (v + 1) * blk].astype(BF16).reshape(part.shape[1:])
             for i in range(1, 3 if square else groups):
                 reduce_part(o, i).start()
+
+    @pl.loop(1, chips)
+    def _(e):
+        start_parts(near(n - 2 * e) // 2)
 
     far_chips = chips - 2
     is_inner = (chip == 1) | (chip == last - 1)
@@ -607,11 +643,11 @@
 
         @pl.when(over & is_end)
         def _():
-            hand(o, next_in * 2 + odd, inbox.at[core, slot], inbox_sem).start()
+            hand(o, next_in * 2 + odd, inbox.at[slot, core], inbox_sem.at[slot]).start()
 
         @pl.when(over & is_inner & (odd != core))
         def _():
-            hand(o, partner, crossed.at[slot], crossed_sem).start()
+            hand(o, partner, crossed.at[slot], crossed_sem.at[slot]).start()
 
         @pl.when(jnp.logical_not(over & (is_end | is_inner)))
         def _():
@@ -627,18 +663,19 @@
         )
 
     def sum_for_far_side():
-        drain(crossed, crossed_sem)
-        drain(inbox, inbox_sem)
         outer = jnp.where(low_side, 0, last)
 
         @pl.loop(0, far_chips)
-        def _(slot):
+        def _(i):
+            slot = jnp.where(low_side, far_chips - 1 - i, i)
+            drain(crossed.at[slot], crossed_sem.at[slot])
+            drain(inbox.at[slot], inbox_sem.at[slot])
             o = jnp.where(low_side, slot + 2, slot) * 2 + core
             terms = (
                 (me, part_sum[o].astype(F32)),
                 (partner, crossed[slot].astype(F32)),
-                (outer * 2, inbox[0, slot].astype(F32)),
-                (outer * 2 + 1, inbox[1, slot].astype(F32)),
+                (outer * 2, inbox[slot, 0].astype(F32)),
+                (outer * 2 + 1, inbox[slot, 1].astype(F32)),
             )
             for k in range(sections):
                 total = None
@@ -678,15 +715,67 @@
 
     relays = both > 0
     weigh(me)
-    gp_arrives(1)
-
-    @pl.when(relays)
-    def _():
-        gp_arrives(2)
-
-    @pl.loop(2, n - 2)
-    def _(j):
-        relayed(far(j))
+
+    def slab_arrives(c):
+        drain(slab(outer_chip * 2 + core, c), slab_sem.at[c])
+        outer = outer_chip * 2 + core
+        across_slab(outer, c).start()
+        ahead = gp_full.at[outer, aligned(mine * span, span, span), columns(c)]
+        pltpu.make_async_remote_copy(
+            src_ref=ahead, dst_ref=ahead,
+            send_sem=sent_sem.at[5], recv_sem=line_sem.at[outer_chip],
+            device_id=(grp, jnp.where(chip == 1, 2, last - 2) * 2 + core), device_id_type=MESH,
+        ).start()
+
+    def help_slab(c):
+        other = outer_chip * 2 + 1 - core
+        drain(slab(other, c), cross_slab_sem.at[c])
+        for r in range(relations):
+            total = None
+            for o in (me, partner, outer_chip * 2 + core, other):
+                product = jnp.dot(msg_end[o, r], gp_full[o, :, c * cut : (c + 1) * cut], preferred_element_type=F32)
+                total = product if total is None else total + product
+            end_send[r, :, c * cut : (c + 1) * cut] = total.astype(BF16)
+        pltpu.make_async_remote_copy(
+            src_ref=end_send.at[:, :, columns(c)], dst_ref=end_recv.at[:, :, columns(c)],
+            send_sem=sent_sem.at[11], recv_sem=help_sem,
+            device_id=(grp, helped * 2 + core), device_id_type=MESH,
+        ).start()
+
+    if sliced:
+        @pl.when(is_end)
+        def _():
+            gp_arrives(1)
+
+            @pl.loop(2, n - 2)
+            def _(j):
+                relayed(far(j))
+
+        @pl.when(jnp.logical_not(is_end))
+        def _():
+            gp_arrives(3 - outward)
+            slab_arrives(0)
+            relayed(far(2))
+            relayed(far(3))
+            gp_crossed(partner)
+            drain(msg_end.at[: 2 * (chips - 2) - 1], end_sem)
+            help_slab(0)
+            slab_arrives(1)
+            relayed(far(4))
+            relayed(far(5))
+            help_slab(1)
+    else:
+        gp_arrives(1)
+
+        @pl.when(relays)
+        def _():
+            gp_arrives(2)
+
+        @pl.loop(2, n - 2)
+        def _(j):
+            relayed(far(j))
+
+    start_parts(chip)
 
     sides = jnp.where(helped == 0, last - chip, chip)
 
@@ -697,9 +786,7 @@
         gp_completes(k)
         gp_crossed(near(2 * k + 1))
 
-    soon = chips == 4
-    outward = jnp.where(chip == 1, 2, 1)
-    if assisted and soon:
+    if assisted and soon and not sliced:
         @pl.when(is_agent)
         def _():
             complete(outward)
@@ -718,9 +805,10 @@
         end_send[...] = end_sum[...].astype(BF16)
         help_end.start()
 
-    if assisted and soon:
+    if assisted and soon and not sliced:
         pl.when(is_agent)(help_out)
 
+    pl.when(is_end)(start_next_messages)
     if not assisted:
         @pl.when(jnp.logical_not(relays))
         def _():
@@ -729,25 +817,35 @@
     relayed(far(n - 2))
     relayed(far(n - 1))
 
-    @pl.when(relays)
-    def _():
-        @pl.loop(3, chips)
-        def _(k):
-            gp_arrives(k)
-
-    relayed(partner)
-    relayed(me)
-
-    @pl.loop(2, n)
-    def _(j):
-        send_reduced(j)
-
-    if not assisted:
-        @pl.when(jnp.logical_not(relays))
+    if not sliced:
+        @pl.when(relays)
         def _():
             @pl.loop(3, chips)
             def _(k):
                 gp_arrives(k)
+
+
+    @pl.loop(2, n - 2)
+    def _(j):
+        send_reduced(j)
+
+    if sliced:
+        pl.when(relays)(lambda: gp_arrives(3))
+
+    relayed(partner)
+    relayed(me)
+    send_reduced(n - 2)
+    send_reduced(n - 1)
+
+    if not assisted:
+        @pl.when(jnp.logical_not(relays))
+        def _():
+            @pl.loop(3, chips)
+            def _(k):
+                gp_arrives(k)
+
+    if assisted:
+        pl.when(is_inner)(sum_for_far_side)
 
     part_sum[partner] = reduced(partner)
     give_partner = pltpu.make_async_remote_copy(
@@ -757,8 +855,6 @@
     )
     give_partner.start()
     part_back[me] = reduced(me)
-    if assisted:
-        pl.when(is_inner)(sum_for_far_side)
 
     if assisted:
         @pl.when(is_end)
@@ -838,7 +934,7 @@
 
         @pl.when(is_end)
         def _():
-            help_end.wait_recv()
+            drain(end_recv, help_sem)
             grad_w[...] = grad_w[...] + end_recv[...].astype(F32)
 
     fetch_pair.wait_send()
@@ -858,7 +954,7 @@
         @pl.when(is_agent)
         def _():
             drain(msg_all.at[: n - 2], sent_sem.at[4])
-            help_end.wait_send()
+            drain(end_send, sent_sem.at[11])
 
         @pl.when(jnp.logical_not(is_agent))
         def _():
@@ -973,13 +1069,13 @@
             pltpu.VMEM((n, 2, quarter, width // 2), BF16),
             pltpu.VMEM((n, quarter, width), BF16),
             pltpu.VMEM((n, quarter, width), BF16),
-            pltpu.VMEM((2, chips - 2, quarter, width), BF16),
+            pltpu.VMEM((chips - 2, 2, quarter, width), BF16),
             pltpu.VMEM((chips - 2, quarter, width), BF16),
             pltpu.VMEM((chips - 2, sections, quarter, width), BF16),
             pltpu.VMEM((2, sections, quarter, width), BF16),
-            dma((4,)), dma((2,)), dma((13,)), dma, dma, dma, dma, dma, dma, dma((2,)),
+            dma((4,)), dma((2,)), dma((13,)), dma, dma, dma, dma, dma((chips - 2,)), dma((chips - 2,)), dma((2,)), dma((2,)), dma((2,)),
             dma((n, 2)), dma((n, 2, 2)),
-            dma((2,)), dma((2,)), dma((n,)), dma((n,)), dma,
+            dma((4,)), dma((4,)), dma((n,)), dma((n,)), dma,
             dma((chips,)), dma((chips,)), dma((chips,)),
         ],
         compiler_params=pltpu.CompilerParams(

time: 65.3 us -> 63.5 us (0.972)
  Pallas kernels: 64.1 us -> 61.9 us
    pallas_call x1, Pallas kernels: 63.2 us -> 61 us  [per_device(): pl.pallas_call(functools.partial(kernel, n, groups), out_shape=(pltpu.VME...]
where the time goes in v5:
time: 63.5 us; the launch traced here: 62.6 us
  Pallas kernels  61.9 us (97%)
  between operations  0.64 us (1%)
    pallas_call x1, Pallas kernels, per_device(): pl.pallas_call(functools.partial(kernel, n, groups), out_shape=(pltpu.VME...  61 us

profile of v5, /device:TPU:1, one launch (start us, length us, event | category | flops | bytes accessed | tf_op | source)
XLA Modules:
  0.0 62.6 jit_solution(674930823003702419)
XLA Ops:
  0.6 61.0 %layer.1 = (bf16[192,256]{1,0:T(8,128)(2,1)S(1)}, f32[2,96,768]{2,1,0:T(8,128)S(1)}, f32[2,32,768]{2,1,0:T(8,128)S(1)}) custom-call(s32[8,8]{1,0:T(8,128)} %table.1, s32[2,2]{1,0:T(2,128)} %counts.1, s32[2,2,8]{2,1,0:T(2,128)} %slots.1, bf16[2,4,32,768]{3,2,1,0:T(8,128)(2,1)} %bitcast.4, bf16[256,768]{1,0:T(8,128)(2,1)} %cot_hbm.1, f32[768]{0:T(1024)} %bias.1, ...), custom_call_target="tpu_custom_call" | custom-call | tf_op jit(solution)/shard_map/layer/pallas_call | solution.py:1027
  61.6 0.9 %hand_over.1 = (bf16[192,256]{1,0:T(8,128)(2,1)}, f32[2,96,768]{2,1,0:T(8,128)}, f32[2,32,768]{2,1,0:T(8,128)}) custom-call(bf16[192,256]{1,0:T(8,128)(2,1)S(1)} %get-tuple-element.9.refs_0_, f32[2,96,768]{2,1,0:T(8,128)S(1)} %get-tuple-element.10.refs_1_, f32[2,32,768]{2,1,0:T(8,128)S(1)} %get-tuple-element.11.refs_2_), custom_call_target="tpu_custom_call" | custom-call | tf_op jit(solution)/shard_map/hand_over/pallas_call | solution.py:1091

commit v6 on v5

--- a/solution.py
+++ b/solution.py
@@ -662,10 +662,10 @@
             device_id=(grp, z * 2 + core), device_id_type=MESH,
         )
 
-    def sum_for_far_side():
+    def sum_for_far_side(first=0, past=far_chips):
         outer = jnp.where(low_side, 0, last)
 
-        @pl.loop(0, far_chips)
+        @pl.loop(first, past)
         def _(i):
             slot = jnp.where(low_side, far_chips - 1 - i, i)
             drain(crossed.at[slot], crossed_sem.at[slot])
@@ -746,10 +746,11 @@
         @pl.when(is_end)
         def _():
             gp_arrives(1)
-
-            @pl.loop(2, n - 2)
-            def _(j):
-                relayed(far(j))
+            relayed(far(2))
+            relayed(far(3))
+            start_next_messages()
+            relayed(far(4))
+            relayed(far(5))
 
         @pl.when(jnp.logical_not(is_end))
         def _():
@@ -808,7 +809,8 @@
     if assisted and soon and not sliced:
         pl.when(is_agent)(help_out)
 
-    pl.when(is_end)(start_next_messages)
+    if not sliced:
+        pl.when(is_end)(start_next_messages)
     if not assisted:
         @pl.when(jnp.logical_not(relays))
         def _():
@@ -828,15 +830,18 @@
     @pl.loop(2, n - 2)
     def _(j):
         send_reduced(j)
-
-    if sliced:
-        pl.when(relays)(lambda: gp_arrives(3))
 
     relayed(partner)
     relayed(me)
     send_reduced(n - 2)
     send_reduced(n - 1)
 
+    if sliced:
+        @pl.when(relays)
+        def _():
+            sum_for_far_side(0, 1)
+            gp_arrives(3)
+
     if not assisted:
         @pl.when(jnp.logical_not(relays))
         def _():
@@ -845,7 +850,40 @@
                 gp_arrives(k)
 
     if assisted:
-        pl.when(is_inner)(sum_for_far_side)
+        pl.when(is_inner)(functools.partial(sum_for_far_side, 1 if sliced else 0))
+
+    if assisted:
+        @pl.when(is_end)
+        def _():
+            drain(msg_all.at[:3], msg_sem)
+
+        @pl.when(jnp.logical_not(is_end))
+        def _():
+            drain(msg_all.at[: n - 1], msg_sem)
+    else:
+        drain(msg_all.at[: n - 1], msg_sem)
+
+    if sliced:
+        @pl.when(is_end)
+        def _():
+            gp_completes(1)
+            gp_crossed(partner)
+            weigh(partner)
+            weigh(near(2))
+
+        @pl.when(jnp.logical_not(is_end))
+        def _():
+            inward = 3 - outward
+
+            @pl.loop(0, 3)
+            def _(i):
+                weigh(jnp.where(i == 0, partner, near(2 * outward + jnp.maximum(i - 1, 0))))
+
+            gp_completes(inward)
+            weigh(near(2 * inward))
+            gp_crossed(near(2 * inward + 1))
+            weigh(near(2 * inward + 1))
+            gp_completes(3)
 
     part_sum[partner] = reduced(partner)
     give_partner = pltpu.make_async_remote_copy(
@@ -856,48 +894,49 @@
     give_partner.start()
     part_back[me] = reduced(me)
 
-    if assisted:
+    if sliced:
         @pl.when(is_end)
         def _():
-            drain(msg_all.at[:3], msg_sem)
+            gp_crossed(near(3))
+            weigh(near(3))
 
         @pl.when(jnp.logical_not(is_end))
         def _():
-            drain(msg_all.at[: n - 1], msg_sem)
+            weigh(near(6))
+            gp_crossed(near(7))
+            weigh(near(7))
     else:
-        drain(msg_all.at[: n - 1], msg_sem)
-
-    reach = jnp.where(is_end, 2, chips) if assisted else chips
-    waited = jnp.where(is_agent, outward, 0) if assisted and soon else 0
-
-    @pl.loop(1, reach)
-    def _(k):
-        @pl.when(k != waited)
-        def _():
-            gp_completes(k)
-
-    @pl.loop(1, reach)
-    def _(k):
-        @pl.when(k != waited)
-        def _():
-            gp_crossed(near(2 * k + 1))
-
-    if assisted and soon:
-        @pl.when(is_end)
-        def _():
+        reach = jnp.where(is_end, 2, chips) if assisted else chips
+        waited = jnp.where(is_agent, outward, 0) if assisted and soon else 0
+
+        @pl.loop(1, reach)
+        def _(k):
+            @pl.when(k != waited)
+            def _():
+                gp_completes(k)
+
+        @pl.loop(1, reach)
+        def _(k):
+            @pl.when(k != waited)
+            def _():
+                gp_crossed(near(2 * k + 1))
+
+        if assisted and soon:
+            @pl.when(is_end)
+            def _():
+                gp_crossed(partner)
+        else:
             gp_crossed(partner)
-    else:
-        gp_crossed(partner)
-
-    weigh(partner)
-
-    @pl.loop(1, reach)
-    def _(k):
-        weigh(near(2 * k))
-        weigh(near(2 * k + 1))
-
-    if assisted and not soon:
-        pl.when(is_agent)(help_out)
+
+        weigh(partner)
+
+        @pl.loop(1, reach)
+        def _(k):
+            weigh(near(2 * k))
+            weigh(near(2 * k + 1))
+
+        if assisted and not soon:
+            pl.when(is_agent)(help_out)
 
     for k in range(sections):
         grad_f[k] = jnp.zeros((quarter, width), F32)

time: 63.5 us -> 62.6 us (0.986); the launches traced: 62.6 us -> 62.5 us
  no operation moved by 1% of the time
where the time goes in v6:
time: 62.6 us; the launch traced here: 62.5 us
  Pallas kernels  61.8 us (99%)
  between operations  0.64 us (1%)
    pallas_call x1, Pallas kernels, per_device(): pl.pallas_call(functools.partial(kernel, n, groups), out_shape=(pltpu.VME...  60.9 us

profile of v6, /device:TPU:1, one launch (start us, length us, event | category | flops | bytes accessed | tf_op | source)
XLA Modules:
  0.0 62.5 jit_solution(16776193364929499530)
XLA Ops:
  0.6 60.9 %layer.1 = (bf16[192,256]{1,0:T(8,128)(2,1)S(1)}, f32[2,96,768]{2,1,0:T(8,128)S(1)}, f32[2,32,768]{2,1,0:T(8,128)S(1)}) custom-call(s32[8,8]{1,0:T(8,128)} %table.1, s32[2,2]{1,0:T(2,128)} %counts.1, s32[2,2,8]{2,1,0:T(2,128)} %slots.1, bf16[2,4,32,768]{3,2,1,0:T(8,128)(2,1)} %bitcast.4, bf16[256,768]{1,0:T(8,128)(2,1)} %cot_hbm.1, f32[768]{0:T(1024)} %bias.1, ...), custom_call_target="tpu_custom_call" | custom-call | tf_op jit(solution)/shard_map/layer/pallas_call | solution.py:1066
  61.5 0.9 %hand_over.1 = (bf16[192,256]{1,0:T(8,128)(2,1)}, f32[2,96,768]{2,1,0:T(8,128)}, f32[2,32,768]{2,1,0:T(8,128)}) custom-call(bf16[192,256]{1,0:T(8,128)(2,1)S(1)} %get-tuple-element.9.refs_0_, f32[2,96,768]{2,1,0:T(8,128)S(1)} %get-tuple-element.10.refs_1_, f32[2,32,768]{2,1,0:T(8,128)S(1)} %get-tuple-element.11.refs_2_), custom_call_target="tpu_custom_call" | custom-call | tf_op jit(solution)/shard_map/hand_over/pallas_call | solution.py:1130

commit v7 on v6

--- a/solution.py
+++ b/solution.py
@@ -188,7 +188,7 @@
         return pltpu.make_async_remote_copy(
             src_ref=fetched.at[rows_at, columns(h)], dst_ref=fetched.at[rows_at, columns(h)],
             send_sem=sent_sem.at[1],
-            recv_sem=b_recv.at[j, h, way] if square and way < 2 else spread_sem,
+            recv_sem=b_recv.at[j, h] if square and way < 2 else spread_sem,
             device_id=(peer, me), device_id_type=MESH,
         )
 
@@ -205,9 +205,8 @@
         j = 2 * k + side
         if not square:
             return
-        spread(j, h, 0).wait_recv()
+        drain(fetched.at[: 2 * quarter, columns(h)], b_recv.at[j, h])
         spread(j, h, 2).start()
-        spread(j, h, 1).wait_recv()
         spread(j, h, 3).start()
 
     def placed(j, h):
@@ -1113,7 +1112,7 @@
             pltpu.VMEM((chips - 2, sections, quarter, width), BF16),
             pltpu.VMEM((2, sections, quarter, width), BF16),
             dma((4,)), dma((2,)), dma((13,)), dma, dma, dma, dma, dma((chips - 2,)), dma((chips - 2,)), dma((2,)), dma((2,)), dma((2,)),
-            dma((n, 2)), dma((n, 2, 2)),
+            dma((n, 2)), dma((n, 2)),
             dma((4,)), dma((4,)), dma((n,)), dma((n,)), dma,
             dma((chips,)), dma((chips,)), dma((chips,)),
         ],

time: 62.6 us -> 62.5 us (level)
  no operation moved by 1% of the time
where the time goes in v7:
time: 62.5 us; the launch traced here: 62.3 us
  Pallas kernels  61.7 us (99%)
  between operations  0.64 us (1%)
    pallas_call x1, Pallas kernels, per_device(): pl.pallas_call(functools.partial(kernel, n, groups), out_shape=(pltpu.VME...  60.8 us

profile of v7, /device:TPU:1, one launch (start us, length us, event | category | flops | bytes accessed | tf_op | source)
XLA Modules:
  0.0 62.3 jit_solution(1145256089732768989)
XLA Ops:
  0.6 60.8 %layer.1 = (bf16[192,256]{1,0:T(8,128)(2,1)S(1)}, f32[2,96,768]{2,1,0:T(8,128)S(1)}, f32[2,32,768]{2,1,0:T(8,128)S(1)}) custom-call(s32[8,8]{1,0:T(8,128)} %table.1, s32[2,2]{1,0:T(2,128)} %counts.1, s32[2,2,8]{2,1,0:T(2,128)} %slots.1, bf16[2,4,32,768]{3,2,1,0:T(8,128)(2,1)} %bitcast.4, bf16[256,768]{1,0:T(8,128)(2,1)} %cot_hbm.1, f32[768]{0:T(1024)} %bias.1, ...), custom_call_target="tpu_custom_call" | custom-call | tf_op jit(solution)/shard_map/layer/pallas_call | solution.py:1065
  61.4 0.9 %hand_over.1 = (bf16[192,256]{1,0:T(8,128)(2,1)}, f32[2,96,768]{2,1,0:T(8,128)}, f32[2,32,768]{2,1,0:T(8,128)}) custom-call(bf16[192,256]{1,0:T(8,128)(2,1)S(1)} %get-tuple-element.9.refs_0_, f32[2,96,768]{2,1,0:T(8,128)S(1)} %get-tuple-element.10.refs_1_, f32[2,32,768]{2,1,0:T(8,128)S(1)} %get-tuple-element.11.refs_2_), custom_call_target="tpu_custom_call" | custom-call | tf_op jit(solution)/shard_map/hand_over/pallas_call | solution.py:1129

commit v8 on v7

--- a/solution.py
+++ b/solution.py
@@ -92,8 +92,8 @@
     load_v = pltpu.make_async_copy(values_hbm, values, load_sem.at[1])
     load_f = pltpu.make_async_copy(feat_hbm, feat, load_sem.at[2])
     load_c = pltpu.make_async_copy(cot_hbm, cot, load_sem.at[3])
+    load_v.start()
     load_f.start()
-    load_v.start()
     load_w.start()
     load_c.start()
 
@@ -351,9 +351,6 @@
     pl.when(jnp.logical_not(is_end))(start_next_messages)
 
     send_messages(partner, chip, msg_all, msg_sem).start()
-    msg_all[me] = msg_t[me]
-    if assisted:
-        msg_end[me] = msg_t[helped * 2 + core]
 
     @pl.loop(0, width // tile_width)
     def _(c):
@@ -385,6 +382,9 @@
         for i in range(1, groups):
             reduce_pre(i, p).start()
 
+    msg_all[me] = msg_t[me]
+    if assisted:
+        msg_end[me] = msg_t[helped * 2 + core]
     load_c.wait()
     for k in range(groups):
         @pl.when(grp == k)

time: 62.5 us -> 62.5 us (level)
  no operation moved by 1% of the time
where the time goes in v8:
time: 62.5 us; the launch traced here: 62.3 us
  Pallas kernels  61.7 us (99%)
  between operations  0.64 us (1%)
    pallas_call x1, Pallas kernels, per_device(): pl.pallas_call(functools.partial(kernel, n, groups), out_shape=(pltpu.VME...  60.7 us

profile of v8, /device:TPU:1, one launch (start us, length us, event | category | flops | bytes accessed | tf_op | source)
XLA Modules:
  0.0 62.3 jit_solution(13416274777687527783)
XLA Ops:
  0.6 60.7 %layer.1 = (bf16[192,256]{1,0:T(8,128)(2,1)S(1)}, f32[2,96,768]{2,1,0:T(8,128)S(1)}, f32[2,32,768]{2,1,0:T(8,128)S(1)}) custom-call(s32[8,8]{1,0:T(8,128)} %table.1, s32[2,2]{1,0:T(2,128)} %counts.1, s32[2,2,8]{2,1,0:T(2,128)} %slots.1, bf16[2,4,32,768]{3,2,1,0:T(8,128)(2,1)} %bitcast.4, bf16[256,768]{1,0:T(8,128)(2,1)} %cot_hbm.1, f32[768]{0:T(1024)} %bias.1, ...), custom_call_target="tpu_custom_call" | custom-call | tf_op jit(solution)/shard_map/layer/pallas_call | solution.py:1065
  61.4 0.9 %hand_over.1 = (bf16[192,256]{1,0:T(8,128)(2,1)}, f32[2,96,768]{2,1,0:T(8,128)}, f32[2,32,768]{2,1,0:T(8,128)}) custom-call(bf16[192,256]{1,0:T(8,128)(2,1)S(1)} %get-tuple-element.9.refs_0_, f32[2,96,768]{2,1,0:T(8,128)S(1)} %get-tuple-element.10.refs_1_, f32[2,32,768]{2,1,0:T(8,128)S(1)} %get-tuple-element.11.refs_2_), custom_call_target="tpu_custom_call" | custom-call | tf_op jit(solution)/shard_map/hand_over/pallas_call | solution.py:1129
